TPU v7x, 512 devices: a whole 4x4x16 slice. The times are simulated.
512 devices in a mesh: row: 128 (over z, x, core), col: 4 (over y).
Axes of the slice: x: 4, y: 4, z: 16, core: 2. Of those that a mesh axis runs over, the one named last changes fastest.
Arguments:
- right_side: float32 [384, 131072], P(None, ('row', 'col')), may hold values from -51 to 51
- leaf_inverse: float32 [512, 256, 256], P(('row', 'col')), may hold values from -0.375 to 0.375
- leaf_diag: float32 [512, 256, 256], P(('row', 'col')), may hold values from -0.375 to 0.375
- node_block: float32 [512, 256, 256], P(('row', 'col')), may hold values from -0.375 to 0.375
Outputs:
- solution: float32 [384, 131072], P(None, ('row', 'col'))
- residual_norm: float32 [384], replicated
All inputs are finite; a program needn't handle non-finite values.
Results may differ from a plain program's by a relative error of at most 0.0001.
Values sent between devices are 32-bit elements; how exact they have to be, the bound alone decides.
No kernel may reach another device: no remote copies, remote signals or barrier semaphores. Data moves between devices by JAX's collectives and lax.ppermute only.
A program may use at most 64 MiB of HBM per device.

v0:
```python
import jax
import jax.numpy as jnp
from jax import lax
from jax.sharding import Mesh
from jax.sharding import PartitionSpec as P

ROW_COL = ("row_0", "row_1", "row_2", "col")
ROW = ("row_0", "row_1", "row_2")


PRECISE = lax.Precision.HIGHEST


def swapped(block, axis, bit):
    count = lax.axis_size(axis)
    route = []
    for low in range(count):
        high = low | 1 << bit
        if high != low and high < count:
            route += [(low, high), (high, low)]
    return lax.ppermute(block, axis, route)


def by_axis(x, axes):
    for axis in axes:
        x = lax.psum(x, axis)
    return x


def apply_block(vectors, block):
    return lax.dot_general(
        vectors,
        block,
        (((1,), (1,)), ((), ())),
        precision=PRECISE,
        preferred_element_type=jnp.float32,
    )


def apply_transpose(vectors, block):
    return jnp.dot(vectors, block, precision=PRECISE, preferred_element_type=jnp.float32)


def bit_of(value, position):
    return value // 2**position % 2


def spread_all(block, device, holder_low, first_bit, last_bit):
    for position in range(first_bit, last_bit):
        partner = swapped(block, ROW_COL, position)
        block = jnp.where(bit_of(device, position) == (holder_low >> position) % 2, block, partner)
    return block


def body(right_side, leaf_inverse, leaf_diag, node_block):
    devices = lax.axis_size(ROW) * lax.axis_size("col")
    tree_depth = devices.bit_length() - 1
    device = lax.axis_index(ROW) * lax.axis_size("col") + lax.axis_index("col")
    leaf_block = leaf_inverse[0]
    own_block = node_block[0]
    half_width = leaf_block.shape[0] // 2
    level_blocks = []
    for tree_level in range(1, tree_depth + 1):
        level_blocks.append(spread_all(own_block, device, 2 ** (tree_level - 1), 0, tree_level))
    root_block = spread_all(own_block, device, 0, 0, tree_depth)
    lifted = apply_block(right_side, leaf_block)
    leaf_part = lifted[:, :half_width]
    skeleton = lifted[:, half_width:]
    stored = []
    merged = lifted
    for tree_level in range(1, tree_depth + 1):
        partner = swapped(skeleton, ROW_COL, tree_level - 1)
        is_left = bit_of(device, tree_level - 1) == 0
        left_part = jnp.where(is_left, skeleton, partner)
        right_part = jnp.where(is_left, partner, skeleton)
        merged = apply_block(
            jnp.concatenate([left_part, right_part], axis=1), level_blocks[tree_level - 1]
        )
        stored.append(merged[:, :half_width])
        skeleton = merged[:, half_width:]
    expanded = apply_block(merged, root_block)
    known = jnp.where(
        bit_of(device, tree_depth - 1) == 0, expanded[:, :half_width], expanded[:, half_width:]
    )
    for tree_level in range(tree_depth - 1, 0, -1):
        expanded = apply_transpose(
            jnp.concatenate([stored[tree_level - 1], known], axis=1), level_blocks[tree_level - 1]
        )
        known = jnp.where(
            bit_of(device, tree_level - 1) == 0, expanded[:, :half_width], expanded[:, half_width:]
        )
    solved = apply_transpose(jnp.concatenate([leaf_part, known], axis=1), leaf_block)
    residual = right_side - apply_block(solved, leaf_diag[0])
    totals = by_axis(jnp.sum(residual * residual, axis=1), ROW_COL)
    residual_norm = jnp.sqrt(totals / (devices * leaf_block.shape[0]) + 1e-06)
    return (solved, residual_norm)


def solution(mesh):
    finer = Mesh(
        mesh.devices.reshape(16, 4, 2, mesh.shape["col"]), ("row_0", "row_1", "row_2", "col")
    )
    placed = (
        P(None, ROW_COL),
        P(ROW_COL, None, None),
        P(ROW_COL, None, None),
        P(ROW_COL, None, None),
    )
    return jax.shard_map(
        body, mesh=finer, in_specs=placed, out_specs=(P(None, ROW_COL), P()), check_vma=False
    )
```

profile of v0, /device:TPU:1, one launch (start us, length us, event | category | flops | bytes accessed | tf_op | source)
XLA Modules:
  0.0 281.4 jit_solution(9956688227786970496)
XLA Ops:
  0.6 0.9 copy-done
  1.6 1.6 fusion.76
  3.2 4.2 %collective-permute-start = (f32[384,128]{0,1:T(8,128)S(1)}, f32[384,128]{0,1:T(8,128)S(1)}, u32[]{:S(2)}, u32[]{:S(2)}) collective-permute-start(f32[384,128]{0,1:T(8,128)S(1)} %slice.145), channel_id=1, source_target_pairs={{0,1},{1,0},{2,3},{3,2},{4,5},{5,4},{6,7},{7,6},{8,9},{9,8},{10,11... | collective-permute-start | bytes 589832 | tf_op jit(solution)/shard_map/ppermute | solution.py:21
  7.4 1.9 collective-permute-start.1
  9.3 1.1 collective-permute-done
  10.4 0.7 broadcast_select_fusion.49
  11.1 3.4 %collective-permute-done.1 = f32[256,256]{1,0:T(8,128)S(1)} collective-permute-done((f32[256,256]{1,0:T(8,128)S(1)}, f32[256,256]{1,0:T(8,128)S(1)}, u32[]{:S(2)}, u32[]{:S(2)}) %collective-permute-start.1) | collective-permute-done | bytes 262176 | tf_op jit(solution)/shard_map/ppermute | solution.py:21
  15.1 7.8 %collective-permute-start.2 = (f32[384,128]{0,1:T(8,128)S(1)}, f32[384,128]{0,1:T(8,128)S(1)}, u32[]{:S(2)}, u32[]{:S(2)}) collective-permute-start(f32[384,128]{0,1:T(8,128)S(1)} %slice.147), channel_id=1, source_target_pairs={{0,2},{2,0},{1,3},{3,1},{4,6},{6,4},{5,7},{7,5},{8,10},{10,8},{9,1... | collective-permute-start | bytes 589832 | tf_op jit(solution)/shard_map/ppermute | solution.py:21
  23.0 1.9 collective-permute-start.3
  24.9 1.0 collective-permute-done.2
  26.7 7.3 %collective-permute-done.3 = f32[256,256]{1,0:T(8,128)S(1)} collective-permute-done((f32[256,256]{1,0:T(8,128)S(1)}, f32[256,256]{1,0:T(8,128)S(1)}, u32[]{:S(2)}, u32[]{:S(2)}) %collective-permute-start.3) | collective-permute-done | bytes 262176 | tf_op jit(solution)/shard_map/ppermute | solution.py:21
  34.6 3.8 %collective-permute-start.4 = (f32[384,128]{0,1:T(8,128)S(1)}, f32[384,128]{0,1:T(8,128)S(1)}, u32[]{:S(2)}, u32[]{:S(2)}) collective-permute-start(f32[384,128]{0,1:T(8,128)S(1)} %slice.149), channel_id=1, source_target_pairs={{0,4},{4,0},{1,5},{5,1},{2,6},{6,2},{3,7},{7,3},{8,12},{12,8},{9,1... | collective-permute-start | bytes 589832 | tf_op jit(solution)/shard_map/ppermute | solution.py:21
  38.5 1.9 collective-permute-start.5
  40.5 0.7 broadcast_select_fusion.45
  41.2 0.7 collective-permute-done.5
  42.6 2.3 collective-permute-start.6
  44.9 2.9 %collective-permute-start.7 = (f32[256,256]{1,0:T(8,128)S(1)}, f32[256,256]{1,0:T(8,128)S(1)}, u32[]{:S(2)}, u32[]{:S(2)}) collective-permute-start(f32[256,256]{1,0:T(8,128)S(1)} %broadcast_select_fusion.9), channel_id=1, source_target_pairs={{0,8},{8,0},{1,9},{9,1},{2,10},{10,2},{3,11},{11,3},{4,12},{12,4},... | collective-permute-start | bytes 786440 | tf_op jit(solution)/shard_map/ppermute | solution.py:21
  47.9 2.8 %collective-permute-done.6 = f32[384,128]{0,1:T(8,128)S(1)} collective-permute-done((f32[384,128]{0,1:T(8,128)S(1)}, f32[384,128]{0,1:T(8,128)S(1)}, u32[]{:S(2)}, u32[]{:S(2)}) %collective-permute-start.6) | collective-permute-done | bytes 196640 | tf_op jit(solution)/shard_map/ppermute | solution.py:21
  50.8 0.7 broadcast_select_fusion.43
  51.5 4.9 %collective-permute-done.7 = f32[256,256]{1,0:T(8,128)S(1)} collective-permute-done((f32[256,256]{1,0:T(8,128)S(1)}, f32[256,256]{1,0:T(8,128)S(1)}, u32[]{:S(2)}, u32[]{:S(2)}) %collective-permute-start.7) | collective-permute-done | bytes 262176 | tf_op jit(solution)/shard_map/ppermute | solution.py:21
  57.0 3.9 %collective-permute-start.8 = (f32[384,128]{0,1:T(8,128)S(1)}, f32[384,128]{0,1:T(8,128)}, u32[]{:S(2)}, u32[]{:S(2)}) collective-permute-start(f32[384,128]{0,1:T(8,128)S(1)} %slice.153), channel_id=1, source_target_pairs={{0,16},{16,0},{1,17},{17,1},{2,18},{18,2},{3,19},{19,3},{4,20},{20... | collective-permute-start | bytes 589832 | tf_op jit(solution)/shard_map/ppermute | solution.py:21
  61.0 2.9 %collective-permute-start.9 = (f32[256,256]{1,0:T(8,128)S(1)}, f32[256,256]{1,0:T(8,128)S(1)}, u32[]{:S(2)}, u32[]{:S(2)}) collective-permute-start(f32[256,256]{1,0:T(8,128)S(1)} %broadcast_select_fusion.7), channel_id=1, source_target_pairs={{0,16},{16,0},{1,17},{17,1},{2,18},{18,2},{3,19},{19,3},{4,20},{20... | collective-permute-start | bytes 786440 | tf_op jit(solution)/shard_map/ppermute | solution.py:21
  63.9 2.1 collective-permute-done.8
  66.0 1.6 broadcast_select_fusion.41
  67.7 3.9 %collective-permute-done.9 = f32[256,256]{1,0:T(8,128)S(1)} collective-permute-done((f32[256,256]{1,0:T(8,128)S(1)}, f32[256,256]{1,0:T(8,128)S(1)}, u32[]{:S(2)}, u32[]{:S(2)}) %collective-permute-start.9) | collective-permute-done | bytes 262176 | tf_op jit(solution)/shard_map/ppermute | solution.py:21
  72.8 3.0 %collective-permute-start.10 = (f32[384,128]{0,1:T(8,128)}, f32[384,128]{0,1:T(8,128)}, u32[]{:S(2)}, u32[]{:S(2)}) collective-permute-start(f32[384,128]{0,1:T(8,128)} %slice.155), channel_id=1, source_target_pairs={{0,32},{32,0},{1,33},{33,1},{2,34},{34,2},{3,35},{35,3},{4,36},{36... | collective-permute-start | bytes 589832 | tf_op jit(solution)/shard_map/ppermute | solution.py:21
  75.9 2.3 collective-permute-start.11
  78.2 1.3 collective-permute-done.10
  79.6 1.6 broadcast_select_fusion.39
  81.2 4.9 %collective-permute-done.11 = f32[256,256]{1,0:T(8,128)S(1)} collective-permute-done((f32[256,256]{1,0:T(8,128)S(1)}, f32[256,256]{1,0:T(8,128)S(1)}, u32[]{:S(2)}, u32[]{:S(2)}) %collective-permute-start.11) | collective-permute-done | bytes 262176 | tf_op jit(solution)/shard_map/ppermute | solution.py:21
  87.4 4.6 %collective-permute-start.12 = (f32[384,128]{0,1:T(8,128)}, f32[384,128]{0,1:T(8,128)}, u32[]{:S(2)}, u32[]{:S(2)}) collective-permute-start(f32[384,128]{0,1:T(8,128)} %slice.157), channel_id=1, source_target_pairs={{0,64},{64,0},{1,65},{65,1},{2,66},{66,2},{3,67},{67,3},{4,68},{68... | collective-permute-start | bytes 589832 | tf_op jit(solution)/shard_map/ppermute | solution.py:21
  92.1 1.9 collective-permute-start.13
  94.0 13.3 %collective-permute-done.12 = f32[384,128]{0,1:T(8,128)} collective-permute-done((f32[384,128]{0,1:T(8,128)}, f32[384,128]{0,1:T(8,128)}, u32[]{:S(2)}, u32[]{:S(2)}) %collective-permute-start.12) | collective-permute-done | bytes 196640 | tf_op jit(solution)/shard_map/ppermute | solution.py:21
  107.3 1.6 broadcast_select_fusion.37
  108.9 3.9 %collective-permute-done.13 = f32[256,256]{1,0:T(8,128)S(1)} collective-permute-done((f32[256,256]{1,0:T(8,128)S(1)}, f32[256,256]{1,0:T(8,128)S(1)}, u32[]{:S(2)}, u32[]{:S(2)}) %collective-permute-start.13) | collective-permute-done | bytes 262176 | tf_op jit(solution)/shard_map/ppermute | solution.py:21
  114.1 8.8 %collective-permute-start.14 = (f32[384,128]{0,1:T(8,128)}, f32[384,128]{0,1:T(8,128)}, u32[]{:S(2)}, u32[]{:S(2)}) collective-permute-start(f32[384,128]{0,1:T(8,128)} %slice.159), channel_id=1, source_target_pairs={{0,128},{128,0},{1,129},{129,1},{2,130},{130,2},{3,131},{131,3},{4... | collective-permute-start | bytes 589832 | tf_op jit(solution)/shard_map/ppermute | solution.py:21
  123.0 1.9 collective-permute-start.15
  124.9 31.5 %collective-permute-done.14 = f32[384,128]{0,1:T(8,128)} collective-permute-done((f32[384,128]{0,1:T(8,128)}, f32[384,128]{0,1:T(8,128)}, u32[]{:S(2)}, u32[]{:S(2)}) %collective-permute-start.14) | collective-permute-done | bytes 196640 | tf_op jit(solution)/shard_map/ppermute | solution.py:21
  156.4 1.6 broadcast_select_fusion.35
  158.0 4.0 %collective-permute-done.15 = f32[256,256]{1,0:T(8,128)} collective-permute-done((f32[256,256]{1,0:T(8,128)S(1)}, f32[256,256]{1,0:T(8,128)}, u32[]{:S(2)}, u32[]{:S(2)}) %collective-permute-start.15) | collective-permute-done | bytes 262176 | tf_op jit(solution)/shard_map/ppermute | solution.py:21
  162.0 1.6 fusion.30
  164.3 16.3 %collective-permute-start.16 = (f32[384,128]{0,1:T(8,128)}, f32[384,128]{0,1:T(8,128)}, u32[]{:S(2)}, u32[]{:S(2)}) collective-permute-start(f32[384,128]{0,1:T(8,128)} %slice.161), channel_id=1, source_target_pairs={{0,256},{256,0},{1,257},{257,1},{2,258},{258,2},{3,259},{259,3},{4... | collective-permute-start | bytes 589832 | tf_op jit(solution)/shard_map/ppermute | solution.py:21
  180.6 0.7 broadcast_select_fusion
  181.3 2.1 collective-permute-start.17
  183.5 1.9 copy.6
  185.4 17.8 %collective-permute-done.16 = f32[384,128]{0,1:T(8,128)} collective-permute-done((f32[384,128]{0,1:T(8,128)}, f32[384,128]{0,1:T(8,128)}, u32[]{:S(2)}, u32[]{:S(2)}) %collective-permute-start.16) | collective-permute-done | bytes 196640 | tf_op jit(solution)/shard_map/ppermute | solution.py:21
  203.2 1.0 broadcast_select_fusion.33
  204.2 7.2 %collective-permute-done.17 = f32[256,256]{1,0:T(8,128)} collective-permute-done((f32[256,256]{1,0:T(8,128)}, f32[256,256]{1,0:T(8,128)}, u32[]{:S(2)}, u32[]{:S(2)}) %collective-permute-start.17) | collective-permute-done | bytes 262176 | tf_op jit(solution)/shard_map/ppermute | solution.py:21
  211.4 1.8 fusion.34
  213.2 1.6 fusion.78
  214.8 1.6 fusion.38
  216.5 0.9 copy-done.9
  218.1 0.9 copy-done.7
  219.8 0.9 copy-done.5
  221.5 0.9 copy-done.3
  223.1 0.9 copy-done.15
  224.7 0.9 copy-done.14
  226.3 0.9 copy-done.13
  227.9 0.9 copy-done.12
  228.7 0.8 fusion.70
  230.6 21.4 %psum.28 = f32[384]{0:T(512)S(1)} all-reduce(f32[384]{0:T(512)S(1)} %fusion.1), channel_id=1, replica_groups=mesh['row_0'=16,'row_1'=4,'row_2'=2,'col'=4] {'row_0'}, use_global_device_ids=true, to_apply=%region_1.2 | all-reduce | flops 384 | bytes 3072 | tf_op jit(solution)/shard_map/psum | solution.py:26
  251.9 9.1 %psum.29 = f32[384]{0:T(512)S(1)} all-reduce(f32[384]{0:T(512)S(1)} %psum.28), channel_id=1, replica_groups=mesh['row_0'=16,'row_1'=4,'row_2'=2,'col'=4] {'row_1'}, use_global_device_ids=true, to_apply=%region_2.3 | all-reduce | flops 384 | bytes 3072 | tf_op jit(solution)/shard_map/psum | solution.py:26
  261.0 11.8 %psum.30 = f32[384]{0:T(512)S(1)} all-reduce(f32[384]{0:T(512)S(1)} %psum.29), channel_id=1, replica_groups=mesh['row_0'=16,'row_1'=4,'row_2'=2,'col'=4] {'row_2'}, use_global_device_ids=true, to_apply=%region_3.4 | all-reduce | flops 384 | bytes 3072 | tf_op jit(solution)/shard_map/psum | solution.py:26
  272.8 8.0 %psum.31 = f32[384]{0:T(512)S(1)} all-reduce(f32[384]{0:T(512)S(1)} %psum.30), channel_id=1, replica_groups=mesh['row_0'=16,'row_1'=4,'row_2'=2,'col'=4] {'col'}, use_global_device_ids=true, to_apply=%region_4.5 | all-reduce | flops 384 | bytes 3072 | tf_op jit(solution)/shard_map/psum | solution.py:26
  (76 shorter events, 14.7 us)
Async XLA Ops:
  0.6 1.0 copy-start
  3.2 4.2 %copy-start.1 = (f32[1,256,256]{2,1,0:T(8,128)S(1)}, f32[1,256,256]{2,1,0:T(8,128)}, u32[]{:S(2)}) copy-start(f32[1,256,256]{2,1,0:T(8,128)} %param.7) | copy-start | bytes 786436
  3.2 7.2 %collective-permute-start = (f32[384,128]{0,1:T(8,128)S(1)}, f32[384,128]{0,1:T(8,128)S(1)}, u32[]{:S(2)}, u32[]{:S(2)}) collective-permute-start(f32[384,128]{0,1:T(8,128)S(1)} %slice.145), channel_id=1, source_target_pairs={{0,1},{1,0},{2,3},{3,2},{4,5},{5,4},{6,7},{7,6},{8,9},{9,8},{10,11... | collective-permute-start | bytes 589832 | tf_op jit(solution)/shard_map/ppermute | solution.py:21
  7.4 7.1 %collective-permute-start.1 = (f32[256,256]{1,0:T(8,128)S(1)}, f32[256,256]{1,0:T(8,128)S(1)}, u32[]{:S(2)}, u32[]{:S(2)}) collective-permute-start(f32[256,256]{1,0:T(8,128)S(1)} %bitcast.21), channel_id=1, source_target_pairs={{0,1},{1,0},{2,3},{3,2},{4,5},{5,4},{6,7},{7,6},{8,9},{9,8},{10,11... | collective-permute-start | bytes 786440 | tf_op jit(solution)/shard_map/ppermute | solution.py:21
  15.1 10.8 %collective-permute-start.2 = (f32[384,128]{0,1:T(8,128)S(1)}, f32[384,128]{0,1:T(8,128)S(1)}, u32[]{:S(2)}, u32[]{:S(2)}) collective-permute-start(f32[384,128]{0,1:T(8,128)S(1)} %slice.147), channel_id=1, source_target_pairs={{0,2},{2,0},{1,3},{3,1},{4,6},{6,4},{5,7},{7,5},{8,10},{10,8},{9,1... | collective-permute-start | bytes 589832 | tf_op jit(solution)/shard_map/ppermute | solution.py:21
  23.0 11.0 %collective-permute-start.3 = (f32[256,256]{1,0:T(8,128)S(1)}, f32[256,256]{1,0:T(8,128)S(1)}, u32[]{:S(2)}, u32[]{:S(2)}) collective-permute-start(f32[256,256]{1,0:T(8,128)S(1)} %broadcast_select_fusion.13), channel_id=1, source_target_pairs={{0,2},{2,0},{1,3},{3,1},{4,6},{6,4},{5,7},{7,5},{8,10},{10,8},{9,1... | collective-permute-start | bytes 786440 | tf_op jit(solution)/shard_map/ppermute | solution.py:21
  34.6 5.8 %collective-permute-start.4 = (f32[384,128]{0,1:T(8,128)S(1)}, f32[384,128]{0,1:T(8,128)S(1)}, u32[]{:S(2)}, u32[]{:S(2)}) collective-permute-start(f32[384,128]{0,1:T(8,128)S(1)} %slice.149), channel_id=1, source_target_pairs={{0,4},{4,0},{1,5},{5,1},{2,6},{6,2},{3,7},{7,3},{8,12},{12,8},{9,1... | collective-permute-start | bytes 589832 | tf_op jit(solution)/shard_map/ppermute | solution.py:21
  38.5 3.4 %collective-permute-start.5 = (f32[256,256]{1,0:T(8,128)S(1)}, f32[256,256]{1,0:T(8,128)S(1)}, u32[]{:S(2)}, u32[]{:S(2)}) collective-permute-start(f32[256,256]{1,0:T(8,128)S(1)} %broadcast_select_fusion.11), channel_id=1, source_target_pairs={{0,4},{4,0},{1,5},{5,1},{2,6},{6,2},{3,7},{7,3},{8,12},{12,8},{9,1... | collective-permute-start | bytes 786440 | tf_op jit(solution)/shard_map/ppermute | solution.py:21
  42.6 8.2 %collective-permute-start.6 = (f32[384,128]{0,1:T(8,128)S(1)}, f32[384,128]{0,1:T(8,128)S(1)}, u32[]{:S(2)}, u32[]{:S(2)}) collective-permute-start(f32[384,128]{0,1:T(8,128)S(1)} %slice.151), channel_id=1, source_target_pairs={{0,8},{8,0},{1,9},{9,1},{2,10},{10,2},{3,11},{11,3},{4,12},{12,4},... | collective-permute-start | bytes 589832 | tf_op jit(solution)/shard_map/ppermute | solution.py:21
  44.9 11.5 %collective-permute-start.7 = (f32[256,256]{1,0:T(8,128)S(1)}, f32[256,256]{1,0:T(8,128)S(1)}, u32[]{:S(2)}, u32[]{:S(2)}) collective-permute-start(f32[256,256]{1,0:T(8,128)S(1)} %broadcast_select_fusion.9), channel_id=1, source_target_pairs={{0,8},{8,0},{1,9},{9,1},{2,10},{10,2},{3,11},{11,3},{4,12},{12,4},... | collective-permute-start | bytes 786440 | tf_op jit(solution)/shard_map/ppermute | solution.py:21
  56.4 4.5 %copy-start.2 = (f32[256,256]{1,0:T(8,128)}, f32[256,256]{1,0:T(8,128)S(1)}, u32[]{:S(2)}) copy-start(f32[256,256]{1,0:T(8,128)S(1)} %collective-permute-done.7) | copy-start | bytes 786436
  57.0 9.0 %collective-permute-start.8 = (f32[384,128]{0,1:T(8,128)S(1)}, f32[384,128]{0,1:T(8,128)}, u32[]{:S(2)}, u32[]{:S(2)}) collective-permute-start(f32[384,128]{0,1:T(8,128)S(1)} %slice.153), channel_id=1, source_target_pairs={{0,16},{16,0},{1,17},{17,1},{2,18},{18,2},{3,19},{19,3},{4,20},{20... | collective-permute-start | bytes 589832 | tf_op jit(solution)/shard_map/ppermute | solution.py:21
  61.0 10.6 %collective-permute-start.9 = (f32[256,256]{1,0:T(8,128)S(1)}, f32[256,256]{1,0:T(8,128)S(1)}, u32[]{:S(2)}, u32[]{:S(2)}) collective-permute-start(f32[256,256]{1,0:T(8,128)S(1)} %broadcast_select_fusion.7), channel_id=1, source_target_pairs={{0,16},{16,0},{1,17},{17,1},{2,18},{18,2},{3,19},{19,3},{4,20},{20... | collective-permute-start | bytes 786440 | tf_op jit(solution)/shard_map/ppermute | solution.py:21
  71.5 4.3 %copy-start.4 = (f32[256,256]{1,0:T(8,128)}, f32[256,256]{1,0:T(8,128)S(1)}, u32[]{:S(2)}) copy-start(f32[256,256]{1,0:T(8,128)S(1)} %collective-permute-done.9) | copy-start | bytes 786436
  72.8 6.7 %collective-permute-start.10 = (f32[384,128]{0,1:T(8,128)}, f32[384,128]{0,1:T(8,128)}, u32[]{:S(2)}, u32[]{:S(2)}) collective-permute-start(f32[384,128]{0,1:T(8,128)} %slice.155), channel_id=1, source_target_pairs={{0,32},{32,0},{1,33},{33,1},{2,34},{34,2},{3,35},{35,3},{4,36},{36... | collective-permute-start | bytes 589832 | tf_op jit(solution)/shard_map/ppermute | solution.py:21
  75.9 10.2 %collective-permute-start.11 = (f32[256,256]{1,0:T(8,128)S(1)}, f32[256,256]{1,0:T(8,128)S(1)}, u32[]{:S(2)}, u32[]{:S(2)}) collective-permute-start(f32[256,256]{1,0:T(8,128)S(1)} %broadcast_select_fusion.5), channel_id=1, source_target_pairs={{0,32},{32,0},{1,33},{33,1},{2,34},{34,2},{3,35},{35,3},{4,36},{36... | collective-permute-start | bytes 786440 | tf_op jit(solution)/shard_map/ppermute | solution.py:21
  86.1 5.9 %copy-start.6 = (f32[256,256]{1,0:T(8,128)}, f32[256,256]{1,0:T(8,128)S(1)}, u32[]{:S(2)}) copy-start(f32[256,256]{1,0:T(8,128)S(1)} %collective-permute-done.11) | copy-start | bytes 786436
  87.4 19.9 %collective-permute-start.12 = (f32[384,128]{0,1:T(8,128)}, f32[384,128]{0,1:T(8,128)}, u32[]{:S(2)}, u32[]{:S(2)}) collective-permute-start(f32[384,128]{0,1:T(8,128)} %slice.157), channel_id=1, source_target_pairs={{0,64},{64,0},{1,65},{65,1},{2,66},{66,2},{3,67},{67,3},{4,68},{68... | collective-permute-start | bytes 589832 | tf_op jit(solution)/shard_map/ppermute | solution.py:21
  92.1 20.7 %collective-permute-start.13 = (f32[256,256]{1,0:T(8,128)S(1)}, f32[256,256]{1,0:T(8,128)S(1)}, u32[]{:S(2)}, u32[]{:S(2)}) collective-permute-start(f32[256,256]{1,0:T(8,128)S(1)} %broadcast_select_fusion.3), channel_id=1, source_target_pairs={{0,64},{64,0},{1,65},{65,1},{2,66},{66,2},{3,67},{67,3},{4,68},{68... | collective-permute-start | bytes 786440 | tf_op jit(solution)/shard_map/ppermute | solution.py:21
  112.8 1.3 copy-start.8
  114.1 42.3 %collective-permute-start.14 = (f32[384,128]{0,1:T(8,128)}, f32[384,128]{0,1:T(8,128)}, u32[]{:S(2)}, u32[]{:S(2)}) collective-permute-start(f32[384,128]{0,1:T(8,128)} %slice.159), channel_id=1, source_target_pairs={{0,128},{128,0},{1,129},{129,1},{2,130},{130,2},{3,131},{131,3},{4... | collective-permute-start | bytes 589832 | tf_op jit(solution)/shard_map/ppermute | solution.py:21
  123.0 39.0 %collective-permute-start.15 = (f32[256,256]{1,0:T(8,128)S(1)}, f32[256,256]{1,0:T(8,128)}, u32[]{:S(2)}, u32[]{:S(2)}) collective-permute-start(f32[256,256]{1,0:T(8,128)S(1)} %broadcast_select_fusion.1), channel_id=1, source_target_pairs={{0,128},{128,0},{1,129},{129,1},{2,130},{130,2},{3,131},{131,3},{4... | collective-permute-start | bytes 786440 | tf_op jit(solution)/shard_map/ppermute | solution.py:21
  164.3 39.0 %collective-permute-start.16 = (f32[384,128]{0,1:T(8,128)}, f32[384,128]{0,1:T(8,128)}, u32[]{:S(2)}, u32[]{:S(2)}) collective-permute-start(f32[384,128]{0,1:T(8,128)} %slice.161), channel_id=1, source_target_pairs={{0,256},{256,0},{1,257},{257,1},{2,258},{258,2},{3,259},{259,3},{4... | collective-permute-start | bytes 589832 | tf_op jit(solution)/shard_map/ppermute | solution.py:21
  181.3 30.1 %collective-permute-start.17 = (f32[256,256]{1,0:T(8,128)}, f32[256,256]{1,0:T(8,128)}, u32[]{:S(2)}, u32[]{:S(2)}) collective-permute-start(f32[256,256]{1,0:T(8,128)} %broadcast_select_fusion), channel_id=1, source_target_pairs={{0,256},{256,0},{1,257},{257,1},{2,258},{258,2},{3,259},{259,3},{4... | collective-permute-start | bytes 786440 | tf_op jit(solution)/shard_map/ppermute | solution.py:21
  216.4 1.0 copy-start.9
  216.4 1.0 copy-start.19
  218.1 1.0 copy-start.7
  218.1 1.0 copy-start.18
  219.7 1.0 copy-start.5
  219.8 1.0 copy-start.17
  221.4 1.0 copy-start.3
  221.4 1.0 copy-start.16
  223.1 0.9 copy-start.15
  224.6 0.9 copy-start.14
  226.2 0.9 copy-start.13
  227.8 0.9 copy-start.12
  228.7 1.0 copy-start.10
  228.7 1.1 copy-start.20
  229.8 0.7 copy-start.11
where the time goes:
time: 283 us; the launch traced here: 281 us
  waiting for transfers between devices  111 us (39%)
  starting transfers between devices  74.5 us (26%)
  blocking collectives  50.3 us (18%)
  matrix products  18.3 us (6%)
  local copies, waits for them, and re-layouts  13.5 us (5%)
  other arithmetic  12.2 us (4%)
    ppermute x18, waiting for transfers between devices, swapped(): return lax.ppermute(block, axis, route)  111 us
    ppermute x18, starting transfers between devices, swapped(): return lax.ppermute(block, axis, route)  74.5 us
    psum x4, blocking collectives, by_axis(): x = lax.psum(x, axis)  50.3 us
    dot_general x12, matrix products, apply_block(): lax.dot_general(vectors, block, (((1,), (1,)), ((), ())), precision=PRECI...  11.4 us
    unnamed x43, local copies, waits for them, and re-layouts  10.7 us
    select_n x9, other arithmetic, body(): left_part = jnp.where(is_left, skeleton, partner)  10.4 us
    dot_general x9, matrix products, apply_transpose(): jnp.dot(vectors, block, precision=PRECISE, preferred_element_type=jnp.flo...  6.93 us
  transfers between devices with their start and end apart: 18, of which 17 were waited for; matrix products, arithmetic and copies ran while one was open for 5% of the time, Pallas kernels for 0%

commit v1 on v0

v1 whole, which is shorter than its diff:
```python
import jax
import jax.numpy as jnp
from jax import lax
from jax.sharding import Mesh
from jax.sharding import PartitionSpec as P


ALL = ("z", "x", "c", "y")
PLANE = ("x", "c", "y")
PRECISE = lax.Precision.HIGHEST


def swapped(block, axis, bit):
    count = lax.axis_size(axis)
    return lax.ppermute(block, axis, [(i, i ^ bit) for i in range(count)])


def direct(parts, axes):
    return lax.all_to_all(parts, axes, 0, 0)


def to_each(value, axes):
    count = lax.axis_size(axes)
    return direct(jnp.broadcast_to(value[None], (count,) + value.shape), axes)


def powers(count):
    return [1 << k for k in range(count.bit_length() - 1)]


def apply_block(vectors, block):
    return lax.dot_general(
        vectors,
        block,
        (((1,), (1,)), ((), ())),
        precision=PRECISE,
        preferred_element_type=jnp.float32,
    )


def apply_transpose(vectors, block):
    return jnp.dot(vectors, block, precision=PRECISE, preferred_element_type=jnp.float32)


def pick(is_left, values, half):
    return jnp.where(is_left, values[:, :half], values[:, half:])


def joined(is_left, own, other):
    return jnp.concatenate(
        [jnp.where(is_left, own, other), jnp.where(is_left, other, own)], axis=1
    )


def body(right_side, leaf_inverse, leaf_diag, node_block):
    z = lax.axis_index("z")
    planes = lax.axis_size("z")
    depth = planes.bit_length() - 1
    members = lax.axis_size(PLANE)
    member = lax.axis_index(PLANE)
    leaf_block = leaf_inverse[0]
    own_block = node_block[0]
    rhs, width = right_side.shape
    half = width // 2

    groups = lax.axis_size("x")
    group = members // groups

    rows = width // members
    scattered = direct(own_block.reshape(members, rows, width), PLANE)
    along = to_each(scattered[0], "z")
    homes = [0] + [(z >> k << k) + (1 << (k - 1)) for k in range(1, depth + 1)]
    slices = [scattered[i * group] for i in range(1, groups)]
    slices += [lax.dynamic_index_in_dim(along, h, 0, False) for h in homes]
    gathered = to_each(jnp.stack(slices), PLANE)
    whole = [gathered[:, k].reshape(width, width) for k in range(len(slices))]
    across, top = [None] + whole[: groups - 1], whole[groups - 1 :]

    chain = own_block
    skeleton = apply_block(right_side, leaf_block[half:])
    leaf_part = apply_block(right_side, leaf_block[:half])
    lower = []
    for axis in ("y", "c"):
        for bit in powers(lax.axis_size(axis)):
            is_left = (lax.axis_index(axis) & bit) == 0
            other_block = swapped(chain, axis, bit)
            block = jnp.where(is_left, other_block, chain)
            chain = jnp.where(is_left, chain, other_block)
            other = swapped(skeleton, axis, bit)
            mine, theirs = pick(is_left, block, half), pick(~is_left, block, half)
            eliminated = apply_block(skeleton, mine[:half]) + apply_block(other, theirs[:half])
            skeleton = apply_block(skeleton, mine[half:]) + apply_block(other, theirs[half:])
            lower.append((is_left, block, eliminated))

    x = lax.axis_index("x")
    share = rhs // members
    shares = skeleton.reshape(groups, group, share, half)
    shares = lax.dynamic_index_in_dim(shares, member % group, 1, False)
    own = [lax.dynamic_index_in_dim(shares, x, 0, False)]
    for m in range(1, groups):
        part = lax.dynamic_index_in_dim(shares, x ^ m, 0, False)
        own.append(swapped(part, "x", m))
    for bit in powers(groups):
        swap = (x & bit) != 0
        own = [jnp.where(swap, own[i ^ bit], own[i]) for i in range(groups)]
    middle = []
    for bit in powers(groups):
        blocks = [across[(2 * i + 1) * bit] for i in range(groups // (2 * bit))]
        merged = [
            apply_block(jnp.concatenate(own[2 * i : 2 * i + 2], axis=1), block)
            for i, block in enumerate(blocks)
        ]
        middle.append((blocks, [m[:, :half] for m in merged]))
        own = [m[:, half:] for m in merged]
    own = own[0]

    sides = [(z >> k & 1) == 0 for k in range(depth)]
    lifts = [own]
    for k in range(1, depth):
        lifts.append(apply_block(lifts[-1], pick(sides[k - 1], top[k][half:], half)))
    distance = z ^ jnp.arange(planes, dtype=jnp.int32)
    sent = jnp.broadcast_to(lifts[0][None], (planes, share, half))
    for k in range(1, depth):
        sent = jnp.where((distance >> k != 0)[:, None, None], lifts[k][None], sent)
    got = direct(sent, "z")
    stored = []
    for k in range(1, depth + 1):
        from_sibling = (distance >> (k - 1)) == 1
        other = jnp.sum(jnp.where(from_sibling[:, None, None], got, 0.0), axis=0)
        merged = apply_block(joined(sides[k - 1], own, other), top[k])
        stored.append(merged[:, :half])
        own = merged[:, half:]
    known = pick(sides[depth - 1], apply_block(merged, top[0]), half)
    for k in range(depth - 1, 0, -1):
        expanded = apply_transpose(jnp.concatenate([stored[k - 1], known], axis=1), top[k])
        known = pick(sides[k - 1], expanded, half)

    known = [known]
    for blocks, parts in reversed(middle):
        expanded = [
            apply_transpose(jnp.concatenate([part, value], axis=1), block)
            for block, part, value in zip(blocks, parts, known)
        ]
        known = [v for e in expanded for v in (e[:, :half], e[:, half:])]
    known = jnp.stack(known)[:, None]
    known = jnp.broadcast_to(known, (groups, group, share, half))
    known = direct(known.reshape(members, share, half), PLANE).reshape(rhs, half)
    for is_left, block, eliminated in reversed(lower):
        expanded = apply_transpose(jnp.concatenate([eliminated, known], axis=1), block)
        known = pick(is_left, expanded, half)
    solved = apply_transpose(jnp.concatenate([leaf_part, known], axis=1), leaf_block)
    residual = right_side - apply_block(solved, leaf_diag[0])
    squares = jnp.sum(residual * residual, axis=1).reshape(-1, 128)
    totals = jnp.sum(to_each(squares, PLANE), axis=0)
    totals = jnp.sum(to_each(totals, "z"), axis=0).reshape(-1)
    residual_norm = jnp.sqrt(totals / (planes * members * width) + 1e-06)
    return (solved, residual_norm)


def solution(mesh):
    finer = Mesh(mesh.devices.reshape(16, 4, 2, mesh.shape["col"]), ALL)
    placed = (P(None, ALL), P(ALL, None, None), P(ALL, None, None), P(ALL, None, None))
    return jax.shard_map(
        body, mesh=finer, in_specs=placed, out_specs=(P(None, ALL), P()), check_vma=False
    )
```

time: 283 us -> 173 us (0.61)
  waiting for transfers between devices: 111 us -> 24.2 us
  blocking collectives: 50.3 us -> 26 us
  starting transfers between devices: 74.5 us -> 80.8 us
  local copies, waits for them, and re-layouts: 13.5 us -> 9.02 us
  matrix products: 18.3 us -> 22.5 us
  other arithmetic: 12.2 us -> 8.37 us
    ppermute x18 -> x9, waiting for transfers between devices: 111 us -> 7.95 us  [swapped(): return lax.ppermute(block, axis, [(i, i ^ bit) for i in range(count)])]
    all_to_all x0 -> x5, starting transfers between devices: none -> 51.1 us  [direct(): return lax.all_to_all(parts, axes, 0, 0)]
    psum x4 -> x0, blocking collectives: 50.3 us -> none  [by_axis(): x = lax.psum(x, axis)]
    ppermute x18 -> x9, starting transfers between devices: 74.5 us -> 29.7 us  [swapped(): return lax.ppermute(block, axis, [(i, i ^ bit) for i in range(count)])]
    all_to_all x0 -> x2, blocking collectives: none -> 26 us  [direct(): return lax.all_to_all(parts, axes, 0, 0)]
    all_to_all x0 -> x5, waiting for transfers between devices: none -> 16.2 us  [direct(): return lax.all_to_all(parts, axes, 0, 0)]
    unnamed x43, local copies, waits for them, and re-layouts: 10.7 us -> 2.75 us
    select_n x26 -> x19, other arithmetic: 11.6 us -> 4.33 us  [the longest x1 1.49 us: body(): sent = jnp.where((distance >> k != 0)[:, None, None], lifts[k][None], sent)]
  transfers between devices with their start and end apart: 18 -> 14, of which waited for: 17 -> 7; matrix products, arithmetic and copies ran while one was open for 5% -> 15% of each run, Pallas kernels for 0% -> 0%
where the time goes in v1:
time: 173 us; the launch traced here: 172 us
  starting transfers between devices  80.8 us (47%)
  blocking collectives  26 us (15%)
  waiting for transfers between devices  24.2 us (14%)
  matrix products  22.5 us (13%)
  local copies, waits for them, and re-layouts  9.02 us (5%)
  other arithmetic  8.37 us (5%)
    all_to_all x5, starting transfers between devices, direct(): return lax.all_to_all(parts, axes, 0, 0)  51.1 us
    ppermute x9, starting transfers between devices, swapped(): return lax.ppermute(block, axis, [(i, i ^ bit) for i in range(count)])  29.7 us
    all_to_all x2, blocking collectives, direct(): return lax.all_to_all(parts, axes, 0, 0)  26 us
    dot_general x26, matrix products, apply_block(): lax.dot_general(vectors, block, (((1,), (1,)), ((), ())), precision=PRECI...  18.6 us
    all_to_all x5, waiting for transfers between devices, direct(): return lax.all_to_all(parts, axes, 0, 0)  16.2 us
    ppermute x9, waiting for transfers between devices, swapped(): return lax.ppermute(block, axis, [(i, i ^ bit) for i in range(count)])  7.95 us
    dot_general x10, matrix products, apply_transpose(): jnp.dot(vectors, block, precision=PRECISE, preferred_element_type=jnp.flo...  3.89 us
  transfers between devices with their start and end apart: 14, of which 7 were waited for; matrix products, arithmetic and copies ran while one was open for 15% of the time, Pallas kernels for 0%

profile of v1, /device:TPU:1, one launch (start us, length us, event | category | flops | bytes accessed | tf_op | source)
XLA Modules:
  0.0 172.2 jit_solution(17354766747878630209)
XLA Ops:
  0.7 4.2 %collective-permute-start = (f32[256,256]{1,0:T(8,128)}, f32[256,256]{1,0:T(8,128)S(1)}, u32[]{:S(2)}, u32[]{:S(2)}) collective-permute-start(f32[256,256]{1,0:T(8,128)} %bitcast.104), channel_id=1, source_target_pairs={{0,1},{1,0},{2,3},{3,2},{4,5},{5,4},{6,7},{7,6},{8,9},{9,8},{10,11... | collective-permute-start | bytes 786440 | tf_op jit(solution)/shard_map/ppermute | solution.py:15
  4.8 8.3 %all-to-all-start = ((f32[32,8,256]{2,1,0:T(8,128)}), f32[32,8,256]{2,1,0:T(8,128)S(1)}, u32[]{:S(2)}, u32[]{:S(2)}) async-start(f32[32,8,256]{2,1,0:T(8,128)} %bitcast.105), calls=%async_computation | async-start | bytes 524288 | tf_op jit(solution)/shard_map/all_to_all | solution.py:19
  13.1 1.5 fusion.34
  14.6 3.3 %collective-permute-start.1 = (f32[384,128]{1,0:T(8,128)S(1)}, f32[384,128]{1,0:T(8,128)S(1)}, u32[]{:S(2)}, u32[]{:S(2)}) collective-permute-start(f32[384,128]{1,0:T(8,128)S(1)} %fusion.34), channel_id=1, source_target_pairs={{0,1},{1,0},{2,3},{3,2},{4,5},{5,4},{6,7},{7,6},{8,9},{9,8},{10,11... | collective-permute-start | bytes 589832 | tf_op jit(solution)/shard_map/ppermute | solution.py:15
  17.9 0.6 fusion.110
  18.5 0.6 shift-right-arithmetic_compare_fusion
  19.1 0.6 fusion.111
  19.7 0.5 fusion.114
  20.2 1.9 %copy.15 = f32[384,256]{0,1:T(8,128)} copy(f32[384,256]{1,0:T(8,128)} %param.4) | data formatting | bytes 786432 | tf_op args[0]
  22.1 1.2 fusion.36
  23.3 0.7 broadcast_in_dim.115
  24.0 14.4 %all-to-all-start.1 = ((f32[16,8,256]{2,1,0:T(8,128)}), f32[16,8,256]{2,1,0:T(8,128)S(1)}, u32[]{:S(2)}, u32[]{:S(2)}) async-start(f32[16,8,256]{2,1,0:T(8,128)} %broadcast_in_dim.115), calls=%async_computation.1 | async-start | bytes 262144 | tf_op jit(solution)/shard_map/all_to_all | solution.py:19
  38.5 4.3 %collective-permute-start.2 = (f32[256,256]{1,0:T(8,128)S(1)}, f32[256,256]{1,0:T(8,128)S(1)}, u32[]{:S(2)}, u32[]{:S(2)}) collective-permute-start(f32[256,256]{1,0:T(8,128)S(1)} %get-tuple-element.11), channel_id=1, source_target_pairs={{0,2},{1,3},{2,0},{3,1},{4,6},{5,7},{6,4},{7,5},{8,10},{9,11},{10,... | collective-permute-start | bytes 786440 | tf_op jit(solution)/shard_map/ppermute | solution.py:15
  42.8 0.3 fusion.58
  43.1 0.3 convolution_add_fusion.4
  43.5 2.5 %collective-permute-start.3 = (f32[384,128]{1,0:T(8,128)S(1)}, f32[384,128]{1,0:T(8,128)}, u32[]{:S(2)}, u32[]{:S(2)}) collective-permute-start(f32[384,128]{1,0:T(8,128)S(1)} %convolution_add_fusion.4), channel_id=1, source_target_pairs={{0,2},{1,3},{2,0},{3,1},{4,6},{5,7},{6,4},{7,5},{8,10},{9,11},{10,... | collective-permute-start | bytes 589832 | tf_op jit(solution)/shard_map/ppermute | solution.py:15
  46.0 0.4 fusion.61
  46.4 1.1 convolution_add_fusion.5
  47.5 1.3 collective-permute-done.2
  48.8 4.3 %collective-permute-start.4 = (f32[256,256]{1,0:T(8,128)S(1)}, f32[256,256]{1,0:T(8,128)}, u32[]{:S(2)}, u32[]{:S(2)}) collective-permute-start(f32[256,256]{1,0:T(8,128)S(1)} %get-tuple-element.9), channel_id=1, source_target_pairs={{0,4},{4,0},{1,5},{5,1},{2,6},{6,2},{3,7},{7,3},{8,12},{12,8},{9,1... | collective-permute-start | bytes 786440 | tf_op jit(solution)/shard_map/ppermute | solution.py:15
  53.2 1.5 broadcast_in_dim.116
  54.8 7.5 %all-to-all-start.2 = ((f32[32,8,8,256]{3,2,1,0:T(8,128)}), f32[32,8,8,256]{3,2,1,0:T(8,128)S(1)}, u32[]{:S(2)}, u32[]{:S(2)}) async-start(f32[32,8,8,256]{3,2,1,0:T(8,128)} %broadcast_in_dim.116), calls=%async_computation.2 | async-start | bytes 4194304 | tf_op jit(solution)/shard_map/all_to_all | solution.py:19
  62.3 1.3 fusion.52
  63.6 0.3 convolution_add_fusion.2
  64.0 2.1 %collective-permute-start.5 = (f32[384,128]{1,0:T(8,128)S(1)}, f32[384,128]{1,0:T(8,128)S(1)}, u32[]{:S(2)}, u32[]{:S(2)}) collective-permute-start(f32[384,128]{1,0:T(8,128)S(1)} %convolution_add_fusion.2), channel_id=1, source_target_pairs={{0,4},{4,0},{1,5},{5,1},{2,6},{6,2},{3,7},{7,3},{8,12},{12,8},{9,1... | collective-permute-start | bytes 589832 | tf_op jit(solution)/shard_map/ppermute | solution.py:15
  66.1 1.0 broadcast_select_fusion
  67.3 0.7 copy-done.8
  68.0 0.3 fusion.46
  68.4 1.0 convolution_add_fusion
  69.4 1.6 reshape.67
  71.0 0.7 dynamic-slice_bitcast_fusion
  71.7 4.6 %collective-permute-start.6 = (f32[12,128]{1,0:T(8,128)S(1)}, f32[12,128]{1,0:T(8,128)S(1)}, u32[]{:S(2)}, u32[]{:S(2)}) collective-permute-start(f32[12,128]{1,0:T(8,128)S(1)} %get-tuple-element.19), channel_id=1, source_target_pairs={{0,24},{8,16},{16,8},{24,0},{1,25},{9,17},{17,9},{25,1},{2,26},{10... | collective-permute-start | bytes 18440 | tf_op jit(solution)/shard_map/ppermute | solution.py:15
  76.4 2.4 %collective-permute-start.7 = (f32[12,128]{1,0:T(8,128)S(1)}, f32[12,128]{1,0:T(8,128)S(1)}, u32[]{:S(2)}, u32[]{:S(2)}) collective-permute-start(f32[12,128]{1,0:T(8,128)S(1)} %get-tuple-element.18), channel_id=1, source_target_pairs={{0,16},{8,24},{16,0},{24,8},{1,17},{9,25},{17,1},{25,9},{2,18},{10... | collective-permute-start | bytes 18440 | tf_op jit(solution)/shard_map/ppermute | solution.py:15
  78.8 2.0 %collective-permute-start.8 = (f32[12,128]{1,0:T(8,128)S(1)}, f32[12,128]{1,0:T(8,128)S(1)}, u32[]{:S(2)}, u32[]{:S(2)}) collective-permute-start(f32[12,128]{1,0:T(8,128)S(1)} %get-tuple-element.17), channel_id=1, source_target_pairs={{0,8},{8,0},{16,24},{24,16},{1,9},{9,1},{17,25},{25,17},{2,10},{10... | collective-permute-start | bytes 18440 | tf_op jit(solution)/shard_map/ppermute | solution.py:15
  80.8 2.0 %fusion.55 = f32[384,128]{0,1:T(8,128)} fusion(f32[384,128]{1,0:T(8,128)} %collective-permute-done.3, f32[256,128]{1,0:T(8,128)} %copy-done.15), kind=kOutput, calls=%fused_computation.95 | convolution fusion | flops 75497472 | bytes 458752 | tf_op jit(solution)/shard_map/dot_general | solution.py:32
  82.8 3.4 %collective-permute-done.6 = f32[12,128]{1,0:T(8,128)S(1)} collective-permute-done((f32[12,128]{1,0:T(8,128)S(1)}, f32[12,128]{1,0:T(8,128)S(1)}, u32[]{:S(2)}, u32[]{:S(2)}) %collective-permute-start.6) | collective-permute-done | bytes 6176 | tf_op jit(solution)/shard_map/ppermute | solution.py:15
  86.2 2.6 %collective-permute-done.7 = f32[12,128]{1,0:T(8,128)S(1)} collective-permute-done((f32[12,128]{1,0:T(8,128)S(1)}, f32[12,128]{1,0:T(8,128)S(1)}, u32[]{:S(2)}, u32[]{:S(2)}) %collective-permute-start.7) | collective-permute-done | bytes 6176 | tf_op jit(solution)/shard_map/ppermute | solution.py:15
  88.8 0.5 collective-permute-done.8
  89.3 1.3 broadcast_select_fusion.12
  90.6 1.0 fusion.23
  91.6 0.3 fusion.25
  91.9 0.7 fusion.133
  93.6 1.5 select_select_fusion
  95.0 11.8 %all-to-all-start.3 = ((f32[16,12,128]{2,1,0:T(8,128)}), f32[16,12,128]{2,1,0:T(8,128)}, u32[]{:S(2)}, u32[]{:S(2)}) async-start(f32[16,12,128]{2,1,0:T(8,128)} %select_select_fusion), calls=%async_computation.3 | async-start | bytes 262144 | tf_op jit(solution)/shard_map/all_to_all | solution.py:19
  106.8 2.0 %convolution_add_fusion.3 = f32[384,128]{0,1:T(8,128)} fusion(f32[384,128]{0,1:T(8,128)} %fusion.55, f32[384,128]{1,0:T(8,128)S(1)} %convolution_add_fusion.4, f32[256,128]{1,0:T(8,128)} %copy-done.13), kind=kOutput, calls=%fused_computation.6 | convolution fusion | flops 75546624 | bytes 655360 | tf_op jit(solution)/shard_map/dot_general | solution.py:32
  108.9 1.3 fusion.49
  110.2 8.7 %all-to-all-done.3 = f32[16,12,128]{2,1,0:T(8,128)} async-done(((f32[16,12,128]{2,1,0:T(8,128)}), f32[16,12,128]{2,1,0:T(8,128)}, u32[]{:S(2)}, u32[]{:S(2)}) %all-to-all-start.3) | async-done | bytes 98336 | tf_op jit(solution)/shard_map/all_to_all | solution.py:19
  118.9 1.1 select_reduce_fusion.3
  120.0 0.3 fusion.29
  120.3 0.3 fusion.31
  121.0 0.3 fusion.19
  121.2 0.3 fusion.18
  123.1 0.7 broadcast_in_dim.129
  123.8 9.2 %all-to-all-start.4 = ((f32[32,12,128]{2,1,0:T(8,128)}), f32[32,12,128]{2,1,0:T(8,128)S(1)}, u32[]{:S(2)}, u32[]{:S(2)}) async-start(f32[32,12,128]{2,1,0:T(8,128)} %bitcast.24), calls=%async_computation.4 | async-start | bytes 524288 | tf_op jit(solution)/shard_map/all_to_all | solution.py:19
  133.0 1.2 convolution_add_fusion.1
  134.3 7.5 %all-to-all-done.4 = f32[32,12,128]{2,1,0:T(8,128)S(1)} async-done(((f32[32,12,128]{2,1,0:T(8,128)}), f32[32,12,128]{2,1,0:T(8,128)S(1)}, u32[]{:S(2)}, u32[]{:S(2)}) %all-to-all-start.4) | async-done | bytes 196640 | tf_op jit(solution)/shard_map/all_to_all | solution.py:19
  142.0 0.6 fusion.2
  142.7 0.6 fusion.6
  143.4 0.6 fusion.10
  144.1 0.8 fusion.14
  144.9 0.6 fusion.1
  145.5 11.2 %all_to_all.35 = f32[32,3,128]{2,1,0:T(4,128)S(1)} all-to-all(f32[32,3,128]{2,1,0:T(4,128)S(1)} %broadcast_in_dim.131), channel_id=1, replica_groups=mesh['z'=16,'x'=4,'c'=2,'y'=4] {'x','c','y'}, dimensions={0} | all-to-all | bytes 98304 | tf_op jit(solution)/shard_map/all_to_all | solution.py:19
  156.8 14.8 %all_to_all.36 = f32[16,3,128]{2,1,0:T(4,128)S(1)} all-to-all(f32[16,3,128]{2,1,0:T(4,128)S(1)} %broadcast_in_dim.132), channel_id=1, replica_groups=mesh['z'=16,'x'=4,'c'=2,'y'=4] {'z'}, dimensions={0} | all-to-all | bytes 49152 | tf_op jit(solution)/shard_map/all_to_all | solution.py:19
  171.6 0.6 sqrt_bitcast_fusion
  (90 shorter events, 3.6 us)
Async XLA Ops:
  0.6 144.2 %copy-start = (f32[1,256,256]{2,1,0:T(8,128)S(1)}, f32[1,256,256]{2,1,0:T(8,128)}, u32[]{:S(2)}) copy-start(f32[1,256,256]{2,1,0:T(8,128)} %param.6) | copy-start | bytes 786436
  0.6 37.8 %copy-start.4 = (f32[1,256,256]{2,1,0:T(8,128)S(1)}, f32[1,256,256]{2,1,0:T(8,128)}, u32[]{:S(2)}) copy-start(f32[1,256,256]{2,1,0:T(8,128)} %param.7) | copy-start | bytes 786436
  0.7 21.5 %copy-start.1 = (f32[384,256]{1,0:T(8,128)S(1)}, f32[384,256]{1,0:T(8,128)}, u32[]{:S(2)}) copy-start(f32[384,256]{1,0:T(8,128)} %param.4) | copy-start | bytes 1179652
  0.7 21.5 %copy-start.5 = (f32[1,256,256]{2,1,0:T(8,128)S(1)}, f32[1,256,256]{2,1,0:T(8,128)}, u32[]{:S(2)}) copy-start(f32[1,256,256]{2,1,0:T(8,128)} %param.5) | copy-start | bytes 786436
  0.7 37.7 %collective-permute-start = (f32[256,256]{1,0:T(8,128)}, f32[256,256]{1,0:T(8,128)S(1)}, u32[]{:S(2)}, u32[]{:S(2)}) collective-permute-start(f32[256,256]{1,0:T(8,128)} %bitcast.104), channel_id=1, source_target_pairs={{0,1},{1,0},{2,3},{3,2},{4,5},{5,4},{6,7},{7,6},{8,9},{9,8},{10,11... | collective-permute-start | bytes 786440 | tf_op jit(solution)/shard_map/ppermute | solution.py:15
  4.8 18.5 %all-to-all-start = ((f32[32,8,256]{2,1,0:T(8,128)}), f32[32,8,256]{2,1,0:T(8,128)S(1)}, u32[]{:S(2)}, u32[]{:S(2)}) async-start(f32[32,8,256]{2,1,0:T(8,128)} %bitcast.105), calls=%async_computation | async-start | bytes 524288 | tf_op jit(solution)/shard_map/all_to_all | solution.py:19
  14.6 28.1 %collective-permute-start.1 = (f32[384,128]{1,0:T(8,128)S(1)}, f32[384,128]{1,0:T(8,128)S(1)}, u32[]{:S(2)}, u32[]{:S(2)}) collective-permute-start(f32[384,128]{1,0:T(8,128)S(1)} %fusion.34), channel_id=1, source_target_pairs={{0,1},{1,0},{2,3},{3,2},{4,5},{5,4},{6,7},{7,6},{8,9},{9,8},{10,11... | collective-permute-start | bytes 589832 | tf_op jit(solution)/shard_map/ppermute | solution.py:15
  24.0 29.1 %all-to-all-start.1 = ((f32[16,8,256]{2,1,0:T(8,128)}), f32[16,8,256]{2,1,0:T(8,128)S(1)}, u32[]{:S(2)}, u32[]{:S(2)}) async-start(f32[16,8,256]{2,1,0:T(8,128)} %broadcast_in_dim.115), calls=%async_computation.1 | async-start | bytes 262144 | tf_op jit(solution)/shard_map/all_to_all | solution.py:19
  38.5 10.3 %collective-permute-start.2 = (f32[256,256]{1,0:T(8,128)S(1)}, f32[256,256]{1,0:T(8,128)S(1)}, u32[]{:S(2)}, u32[]{:S(2)}) collective-permute-start(f32[256,256]{1,0:T(8,128)S(1)} %get-tuple-element.11), channel_id=1, source_target_pairs={{0,2},{1,3},{2,0},{3,1},{4,6},{5,7},{6,4},{7,5},{8,10},{9,11},{10,... | collective-permute-start | bytes 786440 | tf_op jit(solution)/shard_map/ppermute | solution.py:15
  43.5 18.8 %collective-permute-start.3 = (f32[384,128]{1,0:T(8,128)S(1)}, f32[384,128]{1,0:T(8,128)}, u32[]{:S(2)}, u32[]{:S(2)}) collective-permute-start(f32[384,128]{1,0:T(8,128)S(1)} %convolution_add_fusion.4), channel_id=1, source_target_pairs={{0,2},{1,3},{2,0},{3,1},{4,6},{5,7},{6,4},{7,5},{8,10},{9,11},{10,... | collective-permute-start | bytes 589832 | tf_op jit(solution)/shard_map/ppermute | solution.py:15
  48.8 6.0 %copy-start.7 = (f32[256,256]{1,0:T(8,128)}, f32[256,256]{1,0:T(8,128)S(1)}, u32[]{:S(2)}) copy-start(f32[256,256]{1,0:T(8,128)S(1)} %get-tuple-element.9) | copy-start | bytes 786436
  48.8 17.3 %collective-permute-start.4 = (f32[256,256]{1,0:T(8,128)S(1)}, f32[256,256]{1,0:T(8,128)}, u32[]{:S(2)}, u32[]{:S(2)}) collective-permute-start(f32[256,256]{1,0:T(8,128)S(1)} %get-tuple-element.9), channel_id=1, source_target_pairs={{0,4},{4,0},{1,5},{5,1},{2,6},{6,2},{3,7},{7,3},{8,12},{12,8},{9,1... | collective-permute-start | bytes 786440 | tf_op jit(solution)/shard_map/ppermute | solution.py:15
  54.8 35.8 %all-to-all-start.2 = ((f32[32,8,8,256]{3,2,1,0:T(8,128)}), f32[32,8,8,256]{3,2,1,0:T(8,128)S(1)}, u32[]{:S(2)}, u32[]{:S(2)}) async-start(f32[32,8,8,256]{3,2,1,0:T(8,128)} %broadcast_in_dim.116), calls=%async_computation.2 | async-start | bytes 4194304 | tf_op jit(solution)/shard_map/all_to_all | solution.py:19
  62.3 1.4 copy-start.15
  62.3 5.0 %copy-start.13 = (f32[256,128]{1,0:T(8,128)}, f32[256,128]{1,0:T(8,128)S(1)}, u32[]{:S(2)}) copy-start(f32[256,128]{1,0:T(8,128)S(1)} %get-tuple-element.22) | copy-start | bytes 393220
  64.0 3.3 %collective-permute-start.5 = (f32[384,128]{1,0:T(8,128)S(1)}, f32[384,128]{1,0:T(8,128)S(1)}, u32[]{:S(2)}, u32[]{:S(2)}) collective-permute-start(f32[384,128]{1,0:T(8,128)S(1)} %convolution_add_fusion.2), channel_id=1, source_target_pairs={{0,4},{4,0},{1,5},{5,1},{2,6},{6,2},{3,7},{7,3},{8,12},{12,8},{9,1... | collective-permute-start | bytes 589832 | tf_op jit(solution)/shard_map/ppermute | solution.py:15
  67.2 1.2 copy-start.14
  67.2 1.2 copy-start.12
  67.3 0.7 copy-start.8
  71.7 14.5 %collective-permute-start.6 = (f32[12,128]{1,0:T(8,128)S(1)}, f32[12,128]{1,0:T(8,128)S(1)}, u32[]{:S(2)}, u32[]{:S(2)}) collective-permute-start(f32[12,128]{1,0:T(8,128)S(1)} %get-tuple-element.19), channel_id=1, source_target_pairs={{0,24},{8,16},{16,8},{24,0},{1,25},{9,17},{17,9},{25,1},{2,26},{10... | collective-permute-start | bytes 18440 | tf_op jit(solution)/shard_map/ppermute | solution.py:15
  76.4 12.4 %collective-permute-start.7 = (f32[12,128]{1,0:T(8,128)S(1)}, f32[12,128]{1,0:T(8,128)S(1)}, u32[]{:S(2)}, u32[]{:S(2)}) collective-permute-start(f32[12,128]{1,0:T(8,128)S(1)} %get-tuple-element.18), channel_id=1, source_target_pairs={{0,16},{8,24},{16,0},{24,8},{1,17},{9,25},{17,1},{25,9},{2,18},{10... | collective-permute-start | bytes 18440 | tf_op jit(solution)/shard_map/ppermute | solution.py:15
  78.8 10.5 %collective-permute-start.8 = (f32[12,128]{1,0:T(8,128)S(1)}, f32[12,128]{1,0:T(8,128)S(1)}, u32[]{:S(2)}, u32[]{:S(2)}) collective-permute-start(f32[12,128]{1,0:T(8,128)S(1)} %get-tuple-element.17), channel_id=1, source_target_pairs={{0,8},{8,0},{16,24},{24,16},{1,9},{9,1},{17,25},{25,17},{2,10},{10... | collective-permute-start | bytes 18440 | tf_op jit(solution)/shard_map/ppermute | solution.py:15
  95.0 23.8 %all-to-all-start.3 = ((f32[16,12,128]{2,1,0:T(8,128)}), f32[16,12,128]{2,1,0:T(8,128)}, u32[]{:S(2)}, u32[]{:S(2)}) async-start(f32[16,12,128]{2,1,0:T(8,128)} %select_select_fusion), calls=%async_computation.3 | async-start | bytes 262144 | tf_op jit(solution)/shard_map/all_to_all | solution.py:19
  118.9 3.7 %copy-start.17 = (f32[12,128]{1,0:T(8,128)S(1)}, f32[12,128]{1,0:T(8,128)}, u32[]{:S(2)}) copy-start(f32[12,128]{1,0:T(8,128)} %get-tuple-element.57) | copy-start | bytes 18436
  118.9 4.0 %copy-start.16 = (f32[12,128]{1,0:T(8,128)S(1)}, f32[12,128]{1,0:T(8,128)}, u32[]{:S(2)}) copy-start(f32[12,128]{1,0:T(8,128)} %get-tuple-element.38) | copy-start | bytes 18436
  123.1 19.6 %copy-start.11 = (f32[384,128]{0,1:T(8,128)S(1)}, f32[384,128]{0,1:T(8,128)}, u32[]{:S(2)}) copy-start(f32[384,128]{0,1:T(8,128)} %convolution_add_fusion.3) | copy-start | bytes 589828
  123.8 18.0 %all-to-all-start.4 = ((f32[32,12,128]{2,1,0:T(8,128)}), f32[32,12,128]{2,1,0:T(8,128)S(1)}, u32[]{:S(2)}, u32[]{:S(2)}) async-start(f32[32,12,128]{2,1,0:T(8,128)} %bitcast.24), calls=%async_computation.4 | async-start | bytes 524288 | tf_op jit(solution)/shard_map/all_to_all | solution.py:19
  134.3 9.1 %copy-start.10 = (f32[384,128]{0,1:T(8,128)S(1)}, f32[384,128]{0,1:T(8,128)}, u32[]{:S(2)}) copy-start(f32[384,128]{0,1:T(8,128)} %convolution_add_fusion.5) | copy-start | bytes 589828
  142.6 1.4 copy-start.6
  142.6 1.4 copy-start.9
  142.7 2.2 %copy-start.2 = (f32[384,256]{0,1:T(8,128)S(1)}, f32[384,256]{0,1:T(8,128)}, u32[]{:S(2)}) copy-start(f32[384,256]{0,1:T(8,128)} %copy.15) | copy-start | bytes 1179652
  144.9 27.4 %copy-start.3 = (f32[384,256]{1,0:T(8,128)}, f32[384,256]{1,0:T(8,128)S(1)}, u32[]{:S(2)}) copy-start(f32[384,256]{1,0:T(8,128)S(1)} %fusion.14) | copy-start | bytes 1179652

commit v2 on v1

v2 whole, which is shorter than its diff:
```python
import functools

import jax
import jax.numpy as jnp
from jax import lax
from jax.experimental import pallas as pl
from jax.experimental.pallas import tpu as pltpu
from jax.sharding import Mesh
from jax.sharding import PartitionSpec as P


ALL = ("z", "x", "c", "y")
PLANE = ("x", "c", "y")
PRECISE = lax.Precision.HIGHEST


def swapped(block, axis, bit):
    count = lax.axis_size(axis)
    return lax.ppermute(block, axis, [(i, i ^ bit) for i in range(count)])


def direct(parts, axes):
    return lax.all_to_all(parts, axes, 0, 0)


def to_each(value, axes):
    count = lax.axis_size(axes)
    return direct(jnp.broadcast_to(value[None], (count,) + value.shape), axes)


def powers(count):
    return [1 << k for k in range(count.bit_length() - 1)]


def apply_block(vectors, block):
    return lax.dot_general(
        vectors,
        block,
        (((1,), (1,)), ((), ())),
        precision=PRECISE,
        preferred_element_type=jnp.float32,
    )


def apply_transpose(vectors, block):
    return jnp.dot(vectors, block, precision=PRECISE, preferred_element_type=jnp.float32)


def pick(is_left, values, half):
    return jnp.where(is_left, values[:, :half], values[:, half:])


LIMIT = 16 * 2**20
COST = pl.CostEstimate(flops=40_000_000, bytes_accessed=3_000_000, transcendentals=0)


def whole(gathered_ref, k):
    block = gathered_ref[:, k]
    return block.reshape(block.shape[0] * block.shape[1], block.shape[2])


def halves(value, half):
    return value[:, :half], value[:, half:]


def beside(first, second):
    return jnp.concatenate([first, second], axis=1)


def rise(groups, planes, *refs):
    own_refs, (gathered_ref, sent_ref, own_ref, middle_ref) = refs[:groups], refs[groups:]
    half = sent_ref.shape[-1]
    x, z = lax.axis_index("x"), lax.axis_index("z")
    own = [ref[...] for ref in own_refs]
    for bit in powers(groups):
        swap = (x & bit) != 0
        own = [jnp.where(swap, own[i ^ bit], own[i]) for i in range(groups)]
    for bit in powers(groups):
        above = []
        for i in range(groups // (2 * bit)):
            node = (2 * i + 1) * bit
            merged = apply_block(beside(own[2 * i], own[2 * i + 1]), whole(gathered_ref, node - 1))
            middle_ref[node - 1], skeleton = halves(merged, half)
            above.append(skeleton)
        own = above
    own_ref[...] = own[0]
    lifts = [own[0]]
    for k in range(1, planes.bit_length() - 1):
        low = whole(gathered_ref, groups - 1 + k)[half:]
        lifts.append(apply_block(lifts[-1], pick((z >> (k - 1) & 1) == 0, low, half)))
    for i in range(planes):
        value = lifts[0]
        for k in range(1, len(lifts)):
            value = jnp.where((z ^ i) >> k != 0, lifts[k], value)
        sent_ref[i] = value


def fall(groups, planes, got_ref, own_ref, middle_ref, gathered_ref, known_ref):
    half = own_ref.shape[-1]
    depth = planes.bit_length() - 1
    z = lax.axis_index("z")
    sides = [(z >> k & 1) == 0 for k in range(depth)]
    own = own_ref[...]
    stored = []
    for k in range(1, depth + 1):
        span = 1 << (k - 1)
        first = ((z >> (k - 1)) ^ 1) << (k - 1)
        other = got_ref[first]
        for i in range(1, span):
            other = other + got_ref[first + i]
        left, right = jnp.where(sides[k - 1], own, other), jnp.where(sides[k - 1], other, own)
        merged = apply_block(beside(left, right), whole(gathered_ref, groups - 1 + k))
        eliminated, own = halves(merged, half)
        stored.append(eliminated)
    count = gathered_ref.shape[0] // 2
    root = gathered_ref[pl.ds((z >> (depth - 1)) * count, count), groups - 1]
    known = apply_block(merged, root.reshape(half, 2 * half))
    for k in range(depth - 1, 0, -1):
        mine = pick(sides[k - 1], whole(gathered_ref, groups - 1 + k), half)
        known = apply_transpose(beside(stored[k - 1], known), mine)
    known = [known]
    for bit in reversed(powers(groups)):
        below = []
        for i, value in enumerate(known):
            node = (2 * i + 1) * bit
            expanded = apply_transpose(
                beside(middle_ref[node - 1], value), whole(gathered_ref, node - 1)
            )
            below += halves(expanded, half)
        known = below
    group = known_ref.shape[0] // groups
    for i, value in enumerate(known):
        for j in range(group):
            known_ref[i * group + j] = value


def body(right_side, leaf_inverse, leaf_diag, node_block):
    z = lax.axis_index("z")
    planes = lax.axis_size("z")
    depth = planes.bit_length() - 1
    members = lax.axis_size(PLANE)
    member = lax.axis_index(PLANE)
    leaf_block = leaf_inverse[0]
    own_block = node_block[0]
    rhs, width = right_side.shape
    half = width // 2

    groups = lax.axis_size("x")
    group = members // groups

    rows = width // members
    scattered = direct(own_block.reshape(members, rows, width), PLANE)
    along = to_each(scattered[0], "z")
    homes = [0] + [(z >> k << k) + (1 << (k - 1)) for k in range(1, depth + 1)]
    slices = [scattered[i * group] for i in range(1, groups)]
    slices += [lax.dynamic_index_in_dim(along, h, 0, False) for h in homes]
    gathered = to_each(jnp.stack(slices), PLANE)

    x = lax.axis_index("x")
    share = rhs // members
    stretch = groups * share
    first = (member % group) * stretch
    chain = halves(own_block, half)
    skeleton = apply_block(right_side, leaf_block[half:])
    leaf_part = apply_block(right_side, leaf_block[:half])
    lower = []
    hops = [(axis, bit) for axis in ("y", "c") for bit in powers(lax.axis_size(axis))]
    for axis, bit in hops:
        is_left = (lax.axis_index(axis) & bit) == 0
        if (axis, bit) == hops[0]:
            other_chain = halves(swapped(own_block, axis, bit), half)
            other = swapped(skeleton, axis, bit)
        else:
            packed = swapped(jnp.concatenate((skeleton,) + chain), axis, bit)
            other = packed[:rhs]
            other_chain = packed[rhs : rhs + width], packed[rhs + width :]
        block = [jnp.where(is_left, o, m) for o, m in zip(other_chain, chain)]
        chain = tuple(jnp.where(is_left, m, o) for o, m in zip(other_chain, chain))
        mine, theirs = jnp.where(is_left, *block), jnp.where(is_left, *reversed(block))
        eliminated = apply_block(skeleton, mine[:half]) + apply_block(other, theirs[:half])
        if (axis, bit) == hops[-1]:
            skeleton = lax.dynamic_slice_in_dim(skeleton, first, stretch, 0)
            other = lax.dynamic_slice_in_dim(other, first, stretch, 0)
        skeleton = apply_block(skeleton, mine[half:]) + apply_block(other, theirs[half:])
        lower.append((mine, eliminated))

    shares = skeleton.reshape(groups, share, half)
    own = [lax.dynamic_index_in_dim(shares, x, 0, False)]
    for m in range(1, groups):
        part = lax.dynamic_index_in_dim(shares, x ^ m, 0, False)
        own.append(swapped(part, "x", m))
    kernel = functools.partial(rise, groups, planes)
    small = jax.ShapeDtypeStruct((groups, share, half), jnp.float32)
    sent, own, middle = pl.pallas_call(
        kernel,
        out_shape=(
            jax.ShapeDtypeStruct((planes, share, half), jnp.float32),
            jax.ShapeDtypeStruct((share, half), jnp.float32),
            small,
        ),
        in_specs=[pl.BlockSpec(memory_space=pltpu.VMEM)] * (groups + 1),
        out_specs=(pl.BlockSpec(memory_space=pltpu.VMEM),) * 3,
        cost_estimate=COST,
        compiler_params=pltpu.CompilerParams(vmem_limit_bytes=LIMIT),
    )(*own, gathered)
    got = direct(sent, "z")
    kernel = functools.partial(fall, groups, planes)
    known = pl.pallas_call(
        kernel,
        out_shape=jax.ShapeDtypeStruct((members, share, half), jnp.float32),
        in_specs=[pl.BlockSpec(memory_space=pltpu.VMEM)] * 4,
        out_specs=pl.BlockSpec(memory_space=pltpu.VMEM),
        cost_estimate=COST,
        compiler_params=pltpu.CompilerParams(vmem_limit_bytes=LIMIT),
    )(got, own, middle, gathered)
    known = direct(known, PLANE).reshape(groups, group, share, half)
    known = jnp.swapaxes(known, 0, 1).reshape(rhs, half)
    for mine, eliminated in reversed(lower):
        known = apply_transpose(eliminated, mine[:half]) + apply_transpose(known, mine[half:])
    solved = apply_transpose(jnp.concatenate([leaf_part, known], axis=1), leaf_block)
    residual = right_side - apply_block(solved, leaf_diag[0])
    squares = jnp.sum(residual * residual, axis=1).reshape(-1, 128)
    totals = jnp.sum(to_each(squares, PLANE), axis=0)
    totals = jnp.sum(to_each(totals, "z"), axis=0).reshape(-1)
    residual_norm = jnp.sqrt(totals / (planes * members * width) + 1e-06)
    return (solved, residual_norm)


def solution(mesh):
    finer = Mesh(mesh.devices.reshape(16, 4, 2, mesh.shape["col"]), ALL)
    placed = (P(None, ALL), P(ALL, None, None), P(ALL, None, None), P(ALL, None, None))
    return jax.shard_map(
        body, mesh=finer, in_specs=placed, out_specs=(P(None, ALL), P()), check_vma=False
    )
```

time: 173 us -> 167 us (0.965)
  waiting for transfers between devices: 24.2 us -> 39.7 us
  starting transfers between devices: 80.8 us -> 65.5 us
  Pallas kernels: 0 us -> 6.48 us
  other arithmetic: 8.37 us -> 2.56 us
  local copies, waits for them, and re-layouts: 9.02 us -> 5.49 us
  matrix products: 22.5 us -> 19 us
    all_to_all x5, waiting for transfers between devices: 16.2 us -> 26.4 us  [direct(): return lax.all_to_all(parts, axes, 0, 0)]
    ppermute x9 -> x7, starting transfers between devices: 29.7 us -> 21.6 us  [swapped(): return lax.ppermute(block, axis, [(i, i ^ bit) for i in range(count)])]
    all_to_all x5, starting transfers between devices: 51.1 us -> 43.9 us  [direct(): return lax.all_to_all(parts, axes, 0, 0)]
    pallas_call x0 -> x2, Pallas kernels: none -> 6.48 us  [the longest x1 3.95 us: body(): pl.pallas_call(kernel, out_shape=jax.ShapeDtypeStruct((members, share, ha...]
    ppermute x9 -> x7, waiting for transfers between devices: 7.95 us -> 13.3 us  [swapped(): return lax.ppermute(block, axis, [(i, i ^ bit) for i in range(count)])]
    select_n x19 -> x3, other arithmetic: 4.33 us -> 0.87 us  [body(): jnp.where(is_left, *block)]
    dot_general x26 -> x15, matrix products: 18.6 us -> 16.2 us  [apply_block(): lax.dot_general(vectors, block, (((1,), (1,)), ((), ())), precision=PRECI...]
    reshape x3, local copies, waits for them, and re-layouts: 1.79 us -> 0.04 us  [the longest x1 0.02 us: body(): known = jnp.swapaxes(known, 0, 1).reshape(rhs, half)]
  transfers between devices with their start and end apart: 14 -> 12, of which waited for: 7 -> 8; matrix products, arithmetic and copies ran while one was open for 15% -> 11% of each run, Pallas kernels for 0% -> 0%
where the time goes in v2:
time: 167 us; the launch traced here: 166 us
  starting transfers between devices  65.5 us (39%)
  waiting for transfers between devices  39.7 us (24%)
  blocking collectives  26 us (16%)
  matrix products  19 us (11%)
  Pallas kernels  6.48 us (4%)
  local copies, waits for them, and re-layouts  5.49 us (3%)
  other arithmetic  2.56 us (2%)
    all_to_all x5, starting transfers between devices, direct(): return lax.all_to_all(parts, axes, 0, 0)  43.9 us
    all_to_all x5, waiting for transfers between devices, direct(): return lax.all_to_all(parts, axes, 0, 0)  26.4 us
    all_to_all x2, blocking collectives, direct(): return lax.all_to_all(parts, axes, 0, 0)  26 us
    ppermute x7, starting transfers between devices, swapped(): return lax.ppermute(block, axis, [(i, i ^ bit) for i in range(count)])  21.6 us
    dot_general x15, matrix products, apply_block(): lax.dot_general(vectors, block, (((1,), (1,)), ((), ())), precision=PRECI...  16.2 us
    ppermute x7, waiting for transfers between devices, swapped(): return lax.ppermute(block, axis, [(i, i ^ bit) for i in range(count)])  13.3 us
    pallas_call x1, Pallas kernels, body(): pl.pallas_call(kernel, out_shape=jax.ShapeDtypeStruct((members, share, ha...  3.95 us
  transfers between devices with their start and end apart: 12, of which 8 were waited for; matrix products, arithmetic and copies ran while one was open for 11% of the time, Pallas kernels for 0%

profile of v2, /device:TPU:1, one launch (start us, length us, event | category | flops | bytes accessed | tf_op | source)
XLA Modules:
  0.0 166.0 jit_solution(2994707143519403899)
XLA Ops:
  0.6 0.0 copy-start
  0.7 10.5 %all-to-all-start = ((f32[32,8,256]{2,1,0:T(8,128)}), f32[32,8,256]{2,1,0:T(8,128)S(1)}, u32[]{:S(2)}, u32[]{:S(2)}) async-start(f32[32,8,256]{2,1,0:T(8,128)} %bitcast.49), calls=%async_computation | async-start | bytes 524288 | tf_op jit(solution)/shard_map/all_to_all | solution.py:23
  11.2 3.3 %collective-permute-start = (f32[256,256]{1,0:T(8,128)}, f32[256,256]{1,0:T(8,128)S(1)}, u32[]{:S(2)}, u32[]{:S(2)}) collective-permute-start(f32[256,256]{1,0:T(8,128)} %bitcast.50), channel_id=1, source_target_pairs={{0,1},{1,0},{2,3},{3,2},{4,5},{5,4},{6,7},{7,6},{8,9},{9,8},{10,11... | collective-permute-start | bytes 786440 | tf_op jit(solution)/shard_map/ppermute | solution.py:19
  14.5 1.5 fusion.12
  16.0 2.0 %collective-permute-start.1 = (f32[384,128]{1,0:T(8,128)S(1)}, f32[384,128]{1,0:T(8,128)S(1)}, u32[]{:S(2)}, u32[]{:S(2)}) collective-permute-start(f32[384,128]{1,0:T(8,128)S(1)} %fusion.12), channel_id=1, source_target_pairs={{0,1},{1,0},{2,3},{3,2},{4,5},{5,4},{6,7},{7,6},{8,9},{9,8},{10,11... | collective-permute-start | bytes 589832 | tf_op jit(solution)/shard_map/ppermute | solution.py:19
  18.0 0.0 copy-start.1
  18.0 0.0 copy-start.9
  18.1 1.2 copy.12
  19.3 0.8 all-to-all-done
  20.1 3.2 %collective-permute-done = f32[256,256]{1,0:T(8,128)S(1)} collective-permute-done((f32[256,256]{1,0:T(8,128)}, f32[256,256]{1,0:T(8,128)S(1)}, u32[]{:S(2)}, u32[]{:S(2)}) %collective-permute-start) | collective-permute-done | bytes 262176 | tf_op jit(solution)/shard_map/ppermute | solution.py:19
  23.4 4.1 %collective-permute-done.1 = f32[384,128]{1,0:T(8,128)S(1)} collective-permute-done((f32[384,128]{1,0:T(8,128)S(1)}, f32[384,128]{1,0:T(8,128)S(1)}, u32[]{:S(2)}, u32[]{:S(2)}) %collective-permute-start.1) | collective-permute-done | bytes 196640 | tf_op jit(solution)/shard_map/ppermute | solution.py:19
  27.5 0.3 fusion.24
  27.9 0.3 copy-done.13
  28.2 0.3 convolution_add_fusion.5
  28.6 4.4 %collective-permute-start.2 = (f32[896,128]{1,0:T(8,128)S(1)}, f32[896,128]{1,0:T(8,128)S(1)}, u32[]{:S(2)}, u32[]{:S(2)}) collective-permute-start(f32[896,128]{1,0:T(8,128)S(1)} %pad_maximum_fusion), channel_id=1, source_target_pairs={{0,2},{1,3},{2,0},{3,1},{4,6},{5,7},{6,4},{7,5},{8,10},{9,11},{10,... | collective-permute-start | bytes 1376264 | tf_op jit(solution)/shard_map/ppermute | solution.py:19
  33.0 0.6 copy-done.21
  33.6 0.7 broadcast_in_dim.13
  34.3 13.0 %all-to-all-start.1 = ((f32[16,8,256]{2,1,0:T(8,128)}), f32[16,8,256]{2,1,0:T(8,128)S(1)}, u32[]{:S(2)}, u32[]{:S(2)}) async-start(f32[16,8,256]{2,1,0:T(8,128)} %broadcast_in_dim.13), calls=%async_computation.1 | async-start | bytes 262144 | tf_op jit(solution)/shard_map/all_to_all | solution.py:23
  47.4 1.2 fusion.14
  48.6 0.0 collective-permute-done.2
  48.6 0.8 broadcast_select_fusion.3
  49.4 9.9 %all-to-all-done.1 = f32[16,8,256]{2,1,0:T(8,128)S(1)} async-done(((f32[16,8,256]{2,1,0:T(8,128)}), f32[16,8,256]{2,1,0:T(8,128)S(1)}, u32[]{:S(2)}, u32[]{:S(2)}) %all-to-all-start.1) | async-done | bytes 131104 | tf_op jit(solution)/shard_map/all_to_all | solution.py:23
  59.3 1.6 broadcast_in_dim.28
  60.9 7.4 %all-to-all-start.2 = ((f32[32,8,8,256]{3,2,1,0:T(8,128)}), f32[32,8,8,256]{3,2,1,0:T(8,128)S(1)}, u32[]{:S(2)}, u32[]{:S(2)}) async-start(f32[32,8,8,256]{3,2,1,0:T(8,128)} %broadcast_in_dim.28), calls=%async_computation.2 | async-start | bytes 4194304 | tf_op jit(solution)/shard_map/all_to_all | solution.py:23
  68.3 0.0 copy-start.14
  68.3 1.3 fusion.8
  69.6 1.2 convolution_add_fusion.2
  70.8 1.0 pad_maximum_fusion.1
  71.8 2.2 %collective-permute-start.3 = (f32[896,128]{1,0:T(8,128)S(1)}, f32[896,128]{1,0:T(8,128)S(1)}, u32[]{:S(2)}, u32[]{:S(2)}) collective-permute-start(f32[896,128]{1,0:T(8,128)S(1)} %pad_maximum_fusion.1), channel_id=1, source_target_pairs={{0,4},{4,0},{1,5},{5,1},{2,6},{6,2},{3,7},{7,3},{8,12},{12,8},{9,1... | collective-permute-start | bytes 1376264 | tf_op jit(solution)/shard_map/ppermute | solution.py:19
  74.1 1.2 fusion.26
  75.2 1.0 convolution_add_fusion.7
  76.2 0.0 collective-permute-done.3
  76.3 0.7 copy-done.12
  77.0 0.2 fusion.18
  77.2 0.2 convolution_add_fusion.8
  77.5 0.2 copy-done.18
  77.7 3.4 %collective-permute-start.4 = (f32[12,128]{1,0:T(8,128)S(1)}, f32[12,128]{1,0:T(8,128)S(1)}, u32[]{:S(2)}, u32[]{:S(2)}) collective-permute-start(f32[12,128]{1,0:T(8,128)S(1)} %get-tuple-element.22), channel_id=1, source_target_pairs={{0,8},{8,0},{16,24},{24,16},{1,9},{9,1},{17,25},{25,17},{2,10},{10... | collective-permute-start | bytes 18440 | tf_op jit(solution)/shard_map/ppermute | solution.py:19
  81.0 4.4 %collective-permute-start.5 = (f32[12,128]{1,0:T(8,128)S(1)}, f32[12,128]{1,0:T(8,128)S(1)}, u32[]{:S(2)}, u32[]{:S(2)}) collective-permute-start(f32[12,128]{1,0:T(8,128)S(1)} %get-tuple-element.21), channel_id=1, source_target_pairs={{0,16},{8,24},{16,0},{24,8},{1,17},{9,25},{17,1},{25,9},{2,18},{10... | collective-permute-start | bytes 18440 | tf_op jit(solution)/shard_map/ppermute | solution.py:19
  85.4 1.9 %collective-permute-start.6 = (f32[12,128]{1,0:T(8,128)S(1)}, f32[12,128]{1,0:T(8,128)S(1)}, u32[]{:S(2)}, u32[]{:S(2)}) collective-permute-start(f32[12,128]{1,0:T(8,128)S(1)} %get-tuple-element.20), channel_id=1, source_target_pairs={{0,24},{8,16},{16,8},{24,0},{1,25},{9,17},{17,9},{25,1},{2,26},{10... | collective-permute-start | bytes 18440 | tf_op jit(solution)/shard_map/ppermute | solution.py:19
  87.4 1.9 %fusion.10 = f32[384,128]{1,0:T(8,128)} fusion(f32[896,128]{1,0:T(8,128)} %copy-done.11, f32[256,128]{1,0:T(8,128)} %copy-done.20), kind=kOutput, calls=%fused_computation.23 | convolution fusion | flops 75497472 | bytes 458752 | tf_op jit(solution)/shard_map/dot_general | solution.py:36
  89.3 5.9 %collective-permute-done.4.refs_1_ = f32[12,128]{1,0:T(8,128)S(1)} collective-permute-done((f32[12,128]{1,0:T(8,128)S(1)}, f32[12,128]{1,0:T(8,128)S(1)}, u32[]{:S(2)}, u32[]{:S(2)}) %collective-permute-start.4) | collective-permute-done | bytes 6176 | tf_op jit(solution)/shard_map/ppermute | solution.py:19
  95.2 0.0 collective-permute-done.5.refs_2_
  95.2 0.2 all-to-all-done.2.refs_4_.gathered_ref
  95.4 2.5 %shard_map.59 = (f32[16,12,128]{2,1,0:T(8,128)}, f32[12,128]{1,0:T(8,128)S(1)}, f32[4,12,128]{2,1,0:T(8,128)S(1)}) custom-call(f32[12,128]{1,0:T(8,128)S(1)} %get-tuple-element.23.refs_0_, f32[12,128]{1,0:T(8,128)S(1)} %collective-permute-done.4.refs_1_, f32[12,128]{1,0:T(8,128)S(1)} %collective-permute-done.5.refs_2_, ...), custom_call_target="tpu_custom_call" | custom-call | flops 40000000 | bytes 3000000 | tf_op jit(solution)/shard_map/pallas_call | solution.py:194
  97.9 3.6 %all-to-all-start.3 = ((f32[16,12,128]{2,1,0:T(8,128)}), f32[16,12,128]{2,1,0:T(8,128)S(1)}, u32[]{:S(2)}, u32[]{:S(2)}) async-start(f32[16,12,128]{2,1,0:T(8,128)} %get-tuple-element.5), calls=%async_computation.3 | async-start | bytes 262144 | tf_op jit(solution)/shard_map/all_to_all | solution.py:23
  101.5 2.0 %convolution_add_fusion.4 = f32[384,128]{1,0:T(8,128)} fusion(f32[384,128]{1,0:T(8,128)} %fusion.10, f32[384,128]{1,0:T(8,128)S(1)} %convolution_add_fusion.5, f32[256,128]{1,0:T(8,128)} %get-tuple-element.10), kind=kOutput, calls=%fused_computation.7 | convolution fusion | flops 75546624 | bytes 655360 | tf_op jit(solution)/shard_map/dot_general | solution.py:36
  103.5 1.9 %fusion.20 = f32[384,128]{1,0:T(8,128)} fusion(f32[256,128]{1,0:T(8,128)} %copy-done.18, f32[896,128]{1,0:T(8,128)} %copy-done.12), kind=kOutput, calls=%fused_computation.43 | convolution fusion | flops 75497472 | bytes 458752 | tf_op jit(solution)/shard_map/dot_general | solution.py:36
  105.4 8.1 %all-to-all-done.3.got_ref = f32[16,12,128]{2,1,0:T(8,128)S(1)} async-done(((f32[16,12,128]{2,1,0:T(8,128)}), f32[16,12,128]{2,1,0:T(8,128)S(1)}, u32[]{:S(2)}, u32[]{:S(2)}) %all-to-all-start.3) | async-done | bytes 98336 | tf_op jit(solution)/shard_map/all_to_all | solution.py:23
  113.5 3.9 %shard_map.60 = f32[32,12,128]{2,1,0:T(8,128)} custom-call(f32[16,12,128]{2,1,0:T(8,128)S(1)} %all-to-all-done.3.got_ref, f32[12,128]{1,0:T(8,128)S(1)} %get-tuple-element.6.own_ref, f32[4,12,128]{2,1,0:T(8,128)S(1)} %get-tuple-element.7.middle_ref, f32[32,8,8,256]{3,2,1,0:T(8,128)S(1)} %all-to-all-done.2.refs_4_.gathered_ref), custom_call_target="tpu_custom_call" | custom-call | flops 40000000 | bytes 3000000 | tf_op jit(solution)/shard_map/pallas_call | solution.py:208
  117.4 9.4 %all-to-all-start.4 = ((f32[32,12,128]{2,1,0:T(8,128)}), f32[32,12,128]{2,1,0:T(8,128)S(1)}, u32[]{:S(2)}, u32[]{:S(2)}) async-start(f32[32,12,128]{2,1,0:T(8,128)} %shard_map.60), calls=%async_computation.4 | async-start | bytes 524288 | tf_op jit(solution)/shard_map/all_to_all | solution.py:23
  126.9 1.3 convolution_add_fusion.1
  128.2 7.5 %all-to-all-done.4 = f32[32,12,128]{2,1,0:T(8,128)S(1)} async-done(((f32[32,12,128]{2,1,0:T(8,128)}), f32[32,12,128]{2,1,0:T(8,128)S(1)}, u32[]{:S(2)}, u32[]{:S(2)}) %all-to-all-start.4) | async-done | bytes 196640 | tf_op jit(solution)/shard_map/all_to_all | solution.py:23
  135.7 0.3 fusion.28
  136.0 0.3 convolution_add_fusion
  136.3 0.3 fusion.33
  136.7 0.3 convolution_add_fusion.3
  137.0 0.4 fusion.38
  137.4 0.4 convolution_add_fusion.6
  137.8 0.8 fusion.2
  138.7 0.0 copy-start.2
  138.7 0.6 fusion.1
  139.3 11.2 %all_to_all.35 = f32[32,3,128]{2,1,0:T(4,128)S(1)} all-to-all(f32[32,3,128]{2,1,0:T(4,128)S(1)} %broadcast_in_dim.30), channel_id=1, replica_groups=mesh['z'=16,'x'=4,'c'=2,'y'=4] {'x','c','y'}, dimensions={0} | all-to-all | bytes 98304 | tf_op jit(solution)/shard_map/all_to_all | solution.py:23
  150.6 14.8 %all_to_all.36 = f32[16,3,128]{2,1,0:T(4,128)S(1)} all-to-all(f32[16,3,128]{2,1,0:T(4,128)S(1)} %broadcast_in_dim.31), channel_id=1, replica_groups=mesh['z'=16,'x'=4,'c'=2,'y'=4] {'z'}, dimensions={0} | all-to-all | bytes 49152 | tf_op jit(solution)/shard_map/all_to_all | solution.py:23
  165.4 0.6 sqrt_bitcast_fusion
  (58 shorter events, 0.4 us)
Async XLA Ops:
  0.6 138.0 %copy-start = (f32[1,256,256]{2,1,0:T(8,128)S(1)}, f32[1,256,256]{2,1,0:T(8,128)}, u32[]{:S(2)}) copy-start(f32[1,256,256]{2,1,0:T(8,128)} %param.6) | copy-start | bytes 786436
  0.6 22.7 %copy-start.8 = (f32[1,256,256]{2,1,0:T(8,128)S(1)}, f32[1,256,256]{2,1,0:T(8,128)}, u32[]{:S(2)}) copy-start(f32[1,256,256]{2,1,0:T(8,128)} %param.7) | copy-start | bytes 786436
  0.7 19.4 %all-to-all-start = ((f32[32,8,256]{2,1,0:T(8,128)}), f32[32,8,256]{2,1,0:T(8,128)S(1)}, u32[]{:S(2)}, u32[]{:S(2)}) async-start(f32[32,8,256]{2,1,0:T(8,128)} %bitcast.49), calls=%async_computation | async-start | bytes 524288 | tf_op jit(solution)/shard_map/all_to_all | solution.py:23
  11.2 12.1 %collective-permute-start = (f32[256,256]{1,0:T(8,128)}, f32[256,256]{1,0:T(8,128)S(1)}, u32[]{:S(2)}, u32[]{:S(2)}) collective-permute-start(f32[256,256]{1,0:T(8,128)} %bitcast.50), channel_id=1, source_target_pairs={{0,1},{1,0},{2,3},{3,2},{4,5},{5,4},{6,7},{7,6},{8,9},{9,8},{10,11... | collective-permute-start | bytes 786440 | tf_op jit(solution)/shard_map/ppermute | solution.py:19
  16.0 11.5 %collective-permute-start.1 = (f32[384,128]{1,0:T(8,128)S(1)}, f32[384,128]{1,0:T(8,128)S(1)}, u32[]{:S(2)}, u32[]{:S(2)}) collective-permute-start(f32[384,128]{1,0:T(8,128)S(1)} %fusion.12), channel_id=1, source_target_pairs={{0,1},{1,0},{2,3},{3,2},{4,5},{5,4},{6,7},{7,6},{8,9},{9,8},{10,11... | collective-permute-start | bytes 589832 | tf_op jit(solution)/shard_map/ppermute | solution.py:19
  18.0 29.3 %copy-start.1 = (f32[384,256]{1,0:T(8,128)S(1)}, f32[384,256]{1,0:T(8,128)}, u32[]{:S(2)}) copy-start(f32[384,256]{1,0:T(8,128)} %param.4) | copy-start | bytes 1179652
  18.0 29.3 %copy-start.9 = (f32[1,256,256]{2,1,0:T(8,128)S(1)}, f32[1,256,256]{2,1,0:T(8,128)}, u32[]{:S(2)}) copy-start(f32[1,256,256]{2,1,0:T(8,128)} %param.5) | copy-start | bytes 786436
  23.3 5.2 %copy-start.19 = (f32[256,128]{1,0:T(8,128)}, f32[256,128]{1,0:T(8,128)S(1)}, u32[]{:S(2)}) copy-start(f32[256,128]{1,0:T(8,128)S(1)} %get-tuple-element.15) | copy-start | bytes 393220
  23.4 51.9 %copy-start.3 = (f32[256,128]{1,0:T(8,128)}, f32[256,128]{1,0:T(8,128)S(1)}, u32[]{:S(2)}) copy-start(f32[256,128]{1,0:T(8,128)S(1)} %get-tuple-element.14) | copy-start | bytes 393220
  27.5 0.7 copy-start.13
  28.6 20.0 %collective-permute-start.2 = (f32[896,128]{1,0:T(8,128)S(1)}, f32[896,128]{1,0:T(8,128)S(1)}, u32[]{:S(2)}, u32[]{:S(2)}) collective-permute-start(f32[896,128]{1,0:T(8,128)S(1)} %pad_maximum_fusion), channel_id=1, source_target_pairs={{0,2},{1,3},{2,0},{3,1},{4,6},{5,7},{6,4},{7,5},{8,10},{9,11},{10,... | collective-permute-start | bytes 1376264 | tf_op jit(solution)/shard_map/ppermute | solution.py:19
  33.0 0.6 copy-start.21
  33.6 25.6 %copy-start.22 = (f32[8,8,256]{2,1,0:T(8,128)S(1)}, f32[8,8,256]{2,1,0:T(8,128)}, u32[]{:S(2)}) copy-start(f32[8,8,256]{2,1,0:T(8,128)} %copy-done.21) | copy-start | bytes 196612
  34.3 25.0 %all-to-all-start.1 = ((f32[16,8,256]{2,1,0:T(8,128)}), f32[16,8,256]{2,1,0:T(8,128)S(1)}, u32[]{:S(2)}, u32[]{:S(2)}) async-start(f32[16,8,256]{2,1,0:T(8,128)} %broadcast_in_dim.13), calls=%async_computation.1 | async-start | bytes 262144 | tf_op jit(solution)/shard_map/all_to_all | solution.py:23
  48.6 12.3 %copy-start.11 = (f32[896,128]{1,0:T(8,128)}, f32[896,128]{1,0:T(8,128)S(1)}, u32[]{:S(2)}) copy-start(f32[896,128]{1,0:T(8,128)S(1)} %collective-permute-done.2) | copy-start | bytes 1376260
  49.4 19.0 %copy-start.20 = (f32[256,128]{1,0:T(8,128)}, f32[256,128]{1,0:T(8,128)S(1)}, u32[]{:S(2)}) copy-start(f32[256,128]{1,0:T(8,128)S(1)} %get-tuple-element.11) | copy-start | bytes 393220
  60.9 34.5 %all-to-all-start.2 = ((f32[32,8,8,256]{3,2,1,0:T(8,128)}), f32[32,8,8,256]{3,2,1,0:T(8,128)S(1)}, u32[]{:S(2)}, u32[]{:S(2)}) async-start(f32[32,8,8,256]{3,2,1,0:T(8,128)} %broadcast_in_dim.28), calls=%async_computation.2 | async-start | bytes 4194304 | tf_op jit(solution)/shard_map/all_to_all | solution.py:23
  68.3 5.8 %copy-start.14 = (f32[384,128]{1,0:T(8,128)S(1)}, f32[384,128]{1,0:T(8,128)}, u32[]{:S(2)}) copy-start(f32[384,128]{1,0:T(8,128)} %copy-done.13) | copy-start | bytes 589828
  68.3 8.0 %copy-start.6 = (f32[256,128]{1,0:T(8,128)S(1)}, f32[256,128]{1,0:T(8,128)}, u32[]{:S(2)}) copy-start(f32[256,128]{1,0:T(8,128)} %get-tuple-element.12) | copy-start | bytes 393220
  68.3 8.0 %copy-start.7 = (f32[256,128]{1,0:T(8,128)S(1)}, f32[256,128]{1,0:T(8,128)}, u32[]{:S(2)}) copy-start(f32[256,128]{1,0:T(8,128)} %get-tuple-element.13) | copy-start | bytes 393220
  71.8 4.4 %collective-permute-start.3 = (f32[896,128]{1,0:T(8,128)S(1)}, f32[896,128]{1,0:T(8,128)S(1)}, u32[]{:S(2)}, u32[]{:S(2)}) collective-permute-start(f32[896,128]{1,0:T(8,128)S(1)} %pad_maximum_fusion.1), channel_id=1, source_target_pairs={{0,4},{4,0},{1,5},{5,1},{2,6},{6,2},{3,7},{7,3},{8,12},{12,8},{9,1... | collective-permute-start | bytes 1376264 | tf_op jit(solution)/shard_map/ppermute | solution.py:19
  76.2 0.8 copy-start.12
  77.0 0.6 copy-start.18
  77.7 17.5 %collective-permute-start.4 = (f32[12,128]{1,0:T(8,128)S(1)}, f32[12,128]{1,0:T(8,128)S(1)}, u32[]{:S(2)}, u32[]{:S(2)}) collective-permute-start(f32[12,128]{1,0:T(8,128)S(1)} %get-tuple-element.22), channel_id=1, source_target_pairs={{0,8},{8,0},{16,24},{24,16},{1,9},{9,1},{17,25},{25,17},{2,10},{10... | collective-permute-start | bytes 18440 | tf_op jit(solution)/shard_map/ppermute | solution.py:19
  81.0 14.2 %collective-permute-start.5 = (f32[12,128]{1,0:T(8,128)S(1)}, f32[12,128]{1,0:T(8,128)S(1)}, u32[]{:S(2)}, u32[]{:S(2)}) collective-permute-start(f32[12,128]{1,0:T(8,128)S(1)} %get-tuple-element.21), channel_id=1, source_target_pairs={{0,16},{8,24},{16,0},{24,8},{1,17},{9,25},{17,1},{25,9},{2,18},{10... | collective-permute-start | bytes 18440 | tf_op jit(solution)/shard_map/ppermute | solution.py:19
  85.4 9.8 %collective-permute-start.6 = (f32[12,128]{1,0:T(8,128)S(1)}, f32[12,128]{1,0:T(8,128)S(1)}, u32[]{:S(2)}, u32[]{:S(2)}) collective-permute-start(f32[12,128]{1,0:T(8,128)S(1)} %get-tuple-element.20), channel_id=1, source_target_pairs={{0,24},{8,16},{16,8},{24,0},{1,25},{9,17},{17,9},{25,1},{2,26},{10... | collective-permute-start | bytes 18440 | tf_op jit(solution)/shard_map/ppermute | solution.py:19
  97.9 15.5 %all-to-all-start.3 = ((f32[16,12,128]{2,1,0:T(8,128)}), f32[16,12,128]{2,1,0:T(8,128)S(1)}, u32[]{:S(2)}, u32[]{:S(2)}) async-start(f32[16,12,128]{2,1,0:T(8,128)} %get-tuple-element.5), calls=%async_computation.3 | async-start | bytes 262144 | tf_op jit(solution)/shard_map/all_to_all | solution.py:23
  117.4 18.9 %copy-start.5 = (f32[256,128]{1,0:T(8,128)S(1)}, f32[256,128]{1,0:T(8,128)}, u32[]{:S(2)}) copy-start(f32[256,128]{1,0:T(8,128)} %get-tuple-element.10) | copy-start | bytes 393220
  117.4 19.2 %copy-start.17 = (f32[384,128]{1,0:T(8,128)S(1)}, f32[384,128]{1,0:T(8,128)}, u32[]{:S(2)}) copy-start(f32[384,128]{1,0:T(8,128)} %convolution_add_fusion.4) | copy-start | bytes 589828
  117.4 19.6 %copy-start.4 = (f32[256,128]{1,0:T(8,128)S(1)}, f32[256,128]{1,0:T(8,128)}, u32[]{:S(2)}) copy-start(f32[256,128]{1,0:T(8,128)} %copy-done.3) | copy-start | bytes 393220
  117.4 18.2 %all-to-all-start.4 = ((f32[32,12,128]{2,1,0:T(8,128)}), f32[32,12,128]{2,1,0:T(8,128)S(1)}, u32[]{:S(2)}, u32[]{:S(2)}) async-start(f32[32,12,128]{2,1,0:T(8,128)} %shard_map.60), calls=%async_computation.4 | async-start | bytes 524288 | tf_op jit(solution)/shard_map/all_to_all | solution.py:23
  126.9 10.6 %copy-start.16 = (f32[384,128]{1,0:T(8,128)S(1)}, f32[384,128]{1,0:T(8,128)}, u32[]{:S(2)}) copy-start(f32[384,128]{1,0:T(8,128)} %convolution_add_fusion.7) | copy-start | bytes 589828
  135.6 2.2 %copy-start.10 = (f32[1,256,256]{2,1,0:T(8,128)S(1)}, f32[1,256,256]{2,1,0:T(8,128)}, u32[]{:S(2)}) copy-start(f32[1,256,256]{2,1,0:T(8,128)} %param.5) | copy-start | bytes 786436
  135.6 2.2 %copy-start.15 = (f32[384,128]{0,1:T(8,128)S(1)}, f32[384,128]{0,1:T(8,128)}, u32[]{:S(2)}) copy-start(f32[384,128]{0,1:T(8,128)} %fusion.14) | copy-start | bytes 589828
  138.7 27.4 %copy-start.2 = (f32[384,256]{1,0:T(8,128)}, f32[384,256]{1,0:T(8,128)S(1)}, u32[]{:S(2)}) copy-start(f32[384,256]{1,0:T(8,128)S(1)} %fusion.2) | copy-start | bytes 1179652

commit v3 on v2

v3 whole, which is shorter than its diff:
```python
import functools

import jax
import jax.numpy as jnp
from jax import lax
from jax.experimental import pallas as pl
from jax.experimental.pallas import tpu as pltpu
from jax.sharding import Mesh
from jax.sharding import PartitionSpec as P


ALL = ("z", "x", "c", "y")
PLANE = ("x", "c", "y")
PRECISE = lax.Precision.HIGHEST


def swapped(block, axis, bit):
    count = lax.axis_size(axis)
    return lax.ppermute(block, axis, [(i, i ^ bit) for i in range(count)])


def direct(parts, axes):
    return lax.all_to_all(parts, axes, 0, 0)


def to_each(value, axes):
    count = lax.axis_size(axes)
    return direct(jnp.broadcast_to(value[None], (count,) + value.shape), axes)


def powers(count):
    return [1 << k for k in range(count.bit_length() - 1)]


def apply_block(vectors, block):
    return lax.dot_general(
        vectors,
        block,
        (((1,), (1,)), ((), ())),
        precision=PRECISE,
        preferred_element_type=jnp.float32,
    )


def apply_transpose(vectors, block):
    return jnp.dot(vectors, block, precision=PRECISE, preferred_element_type=jnp.float32)


def pick(is_left, values, half):
    return jnp.where(is_left, values[:, :half], values[:, half:])


LIMIT = 16 * 2**20
COST = pl.CostEstimate(flops=40_000_000, bytes_accessed=3_000_000, transcendentals=0)


def rows_of(ref, k):
    block = ref[:, k]
    return block.reshape(block.shape[0] * block.shape[1], block.shape[2])


def halves(value, half):
    return value[:, :half], value[:, half:]


def beside(first, second):
    return jnp.concatenate([first, second], axis=1)


def by_core(compute, mine_ref, theirs_ref):
    core = lax.axis_index("c")
    for owner, refs in ((0, (mine_ref, theirs_ref)), (1, (theirs_ref, mine_ref))):
        pl.when(core == owner)(functools.partial(compute, *refs))


def rise(groups, planes, *refs):
    own_refs = refs[:groups]
    mine_ref, theirs_ref, sent_ref, own_ref, middle_ref = refs[groups:]
    half = sent_ref.shape[-1]
    x, z = lax.axis_index("x"), lax.axis_index("z")

    def compute(upper_ref, lower_ref):
        own = [ref[...] for ref in own_refs]
        for bit in powers(groups):
            swap = (x & bit) != 0
            own = [jnp.where(swap, own[i ^ bit], own[i]) for i in range(groups)]
        for bit in powers(groups):
            above = []
            for i in range(groups // (2 * bit)):
                node = (2 * i + 1) * bit - 1
                joint = beside(own[2 * i], own[2 * i + 1])
                middle_ref[node] = apply_block(joint, rows_of(upper_ref, node))
                above.append(apply_block(joint, rows_of(lower_ref, node)))
            own = above
        own_ref[...] = own[0]
        lifts = [own[0]]
        for k in range(1, planes.bit_length() - 1):
            low = pick((z >> (k - 1) & 1) == 0, rows_of(lower_ref, groups - 1 + k), half)
            lifts.append(apply_block(lifts[-1], low))
        for i in range(planes):
            value = lifts[0]
            for k in range(1, len(lifts)):
                value = jnp.where((z ^ i) >> k != 0, lifts[k], value)
            sent_ref[i] = value

    by_core(compute, mine_ref, theirs_ref)


def fall(groups, planes, got_ref, own_ref, middle_ref, mine_ref, theirs_ref, known_ref):
    half = own_ref.shape[-1]
    depth = planes.bit_length() - 1
    group = known_ref.shape[0] // groups
    z = lax.axis_index("z")
    sides = [(z >> k & 1) == 0 for k in range(depth)]

    def compute(upper_ref, lower_ref):
        own = own_ref[...]
        stored = []
        for k in range(1, depth + 1):
            start = ((z >> (k - 1)) ^ 1) << (k - 1)
            other = got_ref[start]
            for i in range(1, 1 << (k - 1)):
                other = other + got_ref[start + i]
            joint = beside(
                jnp.where(sides[k - 1], own, other), jnp.where(sides[k - 1], other, own)
            )
            stored.append(apply_block(joint, rows_of(upper_ref, groups - 1 + k)))
            own = apply_block(joint, rows_of(lower_ref, groups - 1 + k))
        upper, lower = rows_of(upper_ref, groups - 1), rows_of(lower_ref, groups - 1)
        root = jnp.where(sides[depth - 1], upper, lower)
        known = apply_block(beside(stored[-1], own), root)
        for k in range(depth - 1, 0, -1):
            upper = pick(sides[k - 1], rows_of(upper_ref, groups - 1 + k), half)
            lower = pick(sides[k - 1], rows_of(lower_ref, groups - 1 + k), half)
            known = apply_transpose(stored[k - 1], upper) + apply_transpose(known, lower)
        known = [known]
        for bit in reversed(powers(groups)):
            below = []
            for i, value in enumerate(known):
                node = (2 * i + 1) * bit - 1
                expanded = apply_transpose(middle_ref[node], rows_of(upper_ref, node))
                expanded = expanded + apply_transpose(value, rows_of(lower_ref, node))
                below += halves(expanded, half)
            known = below
        for i, value in enumerate(known):
            for j in range(group):
                known_ref[j * groups + i] = value

    by_core(compute, mine_ref, theirs_ref)


def body(right_side, leaf_inverse, leaf_diag, node_block):
    z = lax.axis_index("z")
    planes = lax.axis_size("z")
    depth = planes.bit_length() - 1
    members = lax.axis_size(PLANE)
    member = lax.axis_index(PLANE)
    leaf_block = leaf_inverse[0]
    own_block = node_block[0]
    rhs, width = right_side.shape
    half = width // 2

    groups = lax.axis_size("x")
    group = members // groups

    rows = width // members
    scattered = direct(own_block.reshape(members, rows, width), ("c", "x", "y"))
    along = to_each(scattered[0], "z")
    homes = [0] + [(z >> k << k) + (1 << (k - 1)) for k in range(1, depth + 1)]
    slices = [scattered[i * lax.axis_size("y")] for i in range(1, groups)]
    slices += [lax.dynamic_index_in_dim(along, h, 0, False) for h in homes]
    blocks = to_each(jnp.stack(slices), ("x", "y"))
    blocks = (blocks, swapped(blocks, "c", 1))

    x = lax.axis_index("x")
    share = rhs // members
    stretch = groups * share
    first = (member % group) * stretch
    chain = own_block
    skeleton = apply_block(right_side, leaf_block[half:])
    leaf_part = apply_block(right_side, leaf_block[:half])
    lower = []
    hops = [(axis, bit) for axis in ("y", "c") for bit in powers(lax.axis_size(axis))]
    for axis, bit in hops:
        is_left = (lax.axis_index(axis) & bit) == 0
        other_chain = swapped(chain, axis, bit)
        other = swapped(skeleton, axis, bit)
        mine = jnp.where(is_left, other_chain[:, :half], chain[:, half:])
        theirs = jnp.where(is_left, other_chain[:, half:], chain[:, :half])
        chain = jnp.where(is_left, chain, other_chain)
        eliminated = apply_block(skeleton, mine[:half]) + apply_block(other, theirs[:half])
        if (axis, bit) == hops[-1]:
            skeleton = lax.dynamic_slice_in_dim(skeleton, first, stretch, 0)
            other = lax.dynamic_slice_in_dim(other, first, stretch, 0)
        skeleton = apply_block(skeleton, mine[half:]) + apply_block(other, theirs[half:])
        lower.append((mine, eliminated))

    shares = skeleton.reshape(groups, share, half)
    own = [lax.dynamic_index_in_dim(shares, x, 0, False)]
    for m in range(1, groups):
        part = lax.dynamic_index_in_dim(shares, x ^ m, 0, False)
        own.append(swapped(part, "x", m))
    kernel = functools.partial(rise, groups, planes)
    small = jax.ShapeDtypeStruct((groups, share, half), jnp.float32)
    sent, own, middle = pl.pallas_call(
        kernel,
        out_shape=(
            jax.ShapeDtypeStruct((planes, share, half), jnp.float32),
            jax.ShapeDtypeStruct((share, half), jnp.float32),
            small,
        ),
        in_specs=[pl.BlockSpec(memory_space=pltpu.VMEM)] * (groups + 2),
        out_specs=(pl.BlockSpec(memory_space=pltpu.VMEM),) * 3,
        cost_estimate=COST,
        compiler_params=pltpu.CompilerParams(vmem_limit_bytes=LIMIT),
    )(*own, *blocks)
    got = direct(sent, "z")
    kernel = functools.partial(fall, groups, planes)
    known = pl.pallas_call(
        kernel,
        out_shape=jax.ShapeDtypeStruct((members, share, half), jnp.float32),
        in_specs=[pl.BlockSpec(memory_space=pltpu.VMEM)] * 5,
        out_specs=pl.BlockSpec(memory_space=pltpu.VMEM),
        cost_estimate=COST,
        compiler_params=pltpu.CompilerParams(vmem_limit_bytes=LIMIT),
    )(got, own, middle, *blocks)
    known = direct(known, ("c", "y", "x")).reshape(rhs, half)
    for mine, eliminated in reversed(lower):
        known = apply_transpose(eliminated, mine[:half]) + apply_transpose(known, mine[half:])
    solved = apply_transpose(jnp.concatenate([leaf_part, known], axis=1), leaf_block)
    residual = right_side - apply_block(solved, leaf_diag[0])
    squares = jnp.sum(residual * residual, axis=1).reshape(-1, 128)
    totals = jnp.sum(to_each(squares, PLANE), axis=0)
    totals = jnp.sum(to_each(totals, "z"), axis=0).reshape(-1)
    residual_norm = jnp.sqrt(totals / (planes * members * width) + 1e-06)
    return (solved, residual_norm)


def solution(mesh):
    finer = Mesh(mesh.devices.reshape(16, 4, 2, mesh.shape["col"]), ALL)
    placed = (P(None, ALL), P(ALL, None, None), P(ALL, None, None), P(ALL, None, None))
    return jax.shard_map(
        body, mesh=finer, in_specs=placed, out_specs=(P(None, ALL), P()), check_vma=False
    )
```

time: 167 us -> 165 us (0.988)
  starting transfers between devices: 65.5 us -> 81.8 us
  waiting for transfers between devices: 39.7 us -> 25.5 us
  matrix products: 19 us -> 15.4 us
    ppermute x7 -> x10, starting transfers between devices: 21.6 us -> 36.5 us  [swapped(): return lax.ppermute(block, axis, [(i, i ^ bit) for i in range(count)])]
    ppermute x7 -> x10, waiting for transfers between devices: 13.3 us -> 0.27 us  [swapped(): return lax.ppermute(block, axis, [(i, i ^ bit) for i in range(count)])]
    dot_general x15, matrix products: 16.2 us -> 12.5 us  [apply_block(): lax.dot_general(vectors, block, (((1,), (1,)), ((), ())), precision=PRECI...]
    unnamed x53 -> x41, local copies, waits for them, and re-layouts: 3.14 us -> 3.44 us
  transfers between devices with their start and end apart: 12 -> 15, of which waited for: 8 -> 5; matrix products, arithmetic and copies ran while one was open for 11% -> 10% of each run, Pallas kernels for 0% -> 0%
where the time goes in v3:
time: 165 us; the launch traced here: 164 us
  starting transfers between devices  81.8 us (50%)
  blocking collectives  26 us (16%)
  waiting for transfers between devices  25.5 us (15%)
  matrix products  15.4 us (9%)
  Pallas kernels  6.3 us (4%)
  local copies, waits for them, and re-layouts  5.26 us (3%)
  other arithmetic  2.62 us (2%)
    all_to_all x5, starting transfers between devices, direct(): return lax.all_to_all(parts, axes, 0, 0)  45.3 us
    ppermute x10, starting transfers between devices, swapped(): return lax.ppermute(block, axis, [(i, i ^ bit) for i in range(count)])  36.5 us
    all_to_all x2, blocking collectives, direct(): return lax.all_to_all(parts, axes, 0, 0)  26 us
    all_to_all x5, waiting for transfers between devices, direct(): return lax.all_to_all(parts, axes, 0, 0)  25.3 us
    dot_general x15, matrix products, apply_block(): lax.dot_general(vectors, block, (((1,), (1,)), ((), ())), precision=PRECI...  12.5 us
    pallas_call x1, Pallas kernels, body(): pl.pallas_call(kernel, out_shape=jax.ShapeDtypeStruct((members, share, ha...  3.84 us
    unnamed x41, local copies, waits for them, and re-layouts  3.44 us
  transfers between devices with their start and end apart: 15, of which 5 were waited for; matrix products, arithmetic and copies ran while one was open for 10% of the time, Pallas kernels for 0%

profile of v3, /device:TPU:1, one launch (start us, length us, event | category | flops | bytes accessed | tf_op | source)
XLA Modules:
  0.0 164.1 jit_solution(3561432732998147185)
XLA Ops:
  0.6 0.0 copy-start
  0.7 10.6 %all-to-all-start = ((f32[32,8,256]{2,1,0:T(8,128)}), f32[32,8,256]{2,1,0:T(8,128)S(1)}, u32[]{:S(2)}, u32[]{:S(2)}) async-start(f32[32,8,256]{2,1,0:T(8,128)} %bitcast.47), calls=%async_computation | async-start | bytes 524288 | tf_op jit(solution)/shard_map/all_to_all | solution.py:23
  11.3 0.0 copy-start.2
  11.3 1.4 fusion.8
  12.7 3.3 %collective-permute-start.1 = (f32[384,128]{1,0:T(8,128)S(1)}, f32[384,128]{1,0:T(8,128)S(1)}, u32[]{:S(2)}, u32[]{:S(2)}) collective-permute-start(f32[384,128]{1,0:T(8,128)S(1)} %fusion.8), channel_id=1, source_target_pairs={{0,1},{1,0},{2,3},{3,2},{4,5},{5,4},{6,7},{7,6},{8,9},{9,8},{10,11... | collective-permute-start | bytes 589832 | tf_op jit(solution)/shard_map/ppermute | solution.py:19
  16.0 2.0 %collective-permute-start = (f32[256,256]{1,0:T(8,128)S(1)}, f32[256,256]{1,0:T(8,128)S(1)}, u32[]{:S(2)}, u32[]{:S(2)}) collective-permute-start(f32[256,256]{1,0:T(8,128)S(1)} %bitcast.48), channel_id=1, source_target_pairs={{0,1},{1,0},{2,3},{3,2},{4,5},{5,4},{6,7},{7,6},{8,9},{9,8},{10,11... | collective-permute-start | bytes 786440 | tf_op jit(solution)/shard_map/ppermute | solution.py:19
  18.1 0.0 copy-start.4
  18.1 0.2 copy.9
  18.3 0.7 copy-done.4
  19.0 1.2 fusion.10
  20.2 0.7 broadcast_in_dim.13
  20.9 13.0 %all-to-all-start.1 = ((f32[16,8,256]{2,1,0:T(8,128)}), f32[16,8,256]{2,1,0:T(8,128)S(1)}, u32[]{:S(2)}, u32[]{:S(2)}) async-start(f32[16,8,256]{2,1,0:T(8,128)} %broadcast_in_dim.13), calls=%async_computation.1 | async-start | bytes 262144 | tf_op jit(solution)/shard_map/all_to_all | solution.py:23
  34.0 0.3 fusion.22
  34.3 0.3 convolution_add_fusion.5
  34.7 4.8 %collective-permute-start.3 = (f32[384,128]{1,0:T(8,128)S(1)}, f32[384,128]{1,0:T(8,128)S(1)}, u32[]{:S(2)}, u32[]{:S(2)}) collective-permute-start(f32[384,128]{1,0:T(8,128)S(1)} %convolution_add_fusion.5), channel_id=1, source_target_pairs={{0,2},{1,3},{2,0},{3,1},{4,6},{5,7},{6,4},{7,5},{8,10},{9,11},{10,... | collective-permute-start | bytes 589832 | tf_op jit(solution)/shard_map/ppermute | solution.py:19
  39.5 2.0 %collective-permute-start.2 = (f32[256,256]{1,0:T(8,128)S(1)}, f32[256,256]{1,0:T(8,128)S(1)}, u32[]{:S(2)}, u32[]{:S(2)}) collective-permute-start(f32[256,256]{1,0:T(8,128)S(1)} %broadcast_select_fusion.1), channel_id=1, source_target_pairs={{0,2},{1,3},{2,0},{3,1},{4,6},{5,7},{6,4},{7,5},{8,10},{9,11},{10,... | collective-permute-start | bytes 786440 | tf_op jit(solution)/shard_map/ppermute | solution.py:19
  41.5 4.4 %all-to-all-done.1 = f32[16,8,256]{2,1,0:T(8,128)S(1)} async-done(((f32[16,8,256]{2,1,0:T(8,128)}), f32[16,8,256]{2,1,0:T(8,128)S(1)}, u32[]{:S(2)}, u32[]{:S(2)}) %all-to-all-start.1) | async-done | bytes 131104 | tf_op jit(solution)/shard_map/all_to_all | solution.py:23
  45.9 1.1 broadcast_in_dim.28
  47.0 6.7 %all-to-all-start.2 = ((f32[16,8,8,256]{3,2,1,0:T(8,128)}), f32[16,8,8,256]{3,2,1,0:T(8,128)S(1)}, u32[]{:S(2)}, u32[]{:S(2)}) async-start(f32[16,8,8,256]{3,2,1,0:T(8,128)} %broadcast_in_dim.28), calls=%async_computation.2 | async-start | bytes 2097152 | tf_op jit(solution)/shard_map/all_to_all | solution.py:23
  53.7 0.3 fusion.24
  54.1 1.0 convolution_add_fusion.7
  55.1 0.7 broadcast_select_fusion
  55.8 5.9 %collective-permute-start.4 = (f32[256,256]{1,0:T(8,128)}, f32[256,256]{1,0:T(8,128)}, u32[]{:S(2)}, u32[]{:S(2)}) collective-permute-start(f32[256,256]{1,0:T(8,128)} %broadcast_select_fusion), channel_id=1, source_target_pairs={{0,4},{4,0},{1,5},{5,1},{2,6},{6,2},{3,7},{7,3},{8,12},{12,8},{9,1... | collective-permute-start | bytes 786440 | tf_op jit(solution)/shard_map/ppermute | solution.py:19
  61.8 1.0 fusion.18
  62.8 3.3 %all-to-all-done.2.refs_4_.mine_ref = f32[16,8,8,256]{3,2,1,0:T(8,128)S(1)} async-done(((f32[16,8,8,256]{3,2,1,0:T(8,128)}), f32[16,8,8,256]{3,2,1,0:T(8,128)S(1)}, u32[]{:S(2)}, u32[]{:S(2)}) %all-to-all-start.2) | async-done | bytes 1048608 | tf_op jit(solution)/shard_map/all_to_all | solution.py:23
  66.0 7.6 %collective-permute-start.9 = (f32[16,8,8,256]{3,2,1,0:T(8,128)S(1)}, f32[16,8,8,256]{3,2,1,0:T(8,128)S(1)}, u32[]{:S(2)}, u32[]{:S(2)}) collective-permute-start(f32[16,8,8,256]{3,2,1,0:T(8,128)S(1)} %all-to-all-done.2.refs_4_.mine_ref), channel_id=1, source_target_pairs={{0,4},{4,0},{1,5},{5,1},{2,6},{6,2},{3,7},{7,3},{8,12},{12,8},{9,1... | collective-permute-start | bytes 3145736 | tf_op jit(solution)/shard_map/ppermute | solution.py:19
  73.7 1.3 convolution_add_fusion.2
  75.0 1.9 %collective-permute-start.5 = (f32[384,128]{1,0:T(8,128)S(1)}, f32[384,128]{1,0:T(8,128)S(1)}, u32[]{:S(2)}, u32[]{:S(2)}) collective-permute-start(f32[384,128]{1,0:T(8,128)S(1)} %convolution_add_fusion.2), channel_id=1, source_target_pairs={{0,4},{4,0},{1,5},{5,1},{2,6},{6,2},{3,7},{7,3},{8,12},{12,8},{9,1... | collective-permute-start | bytes 589832 | tf_op jit(solution)/shard_map/ppermute | solution.py:19
  76.9 1.1 slice_select_fusion.1
  78.0 0.2 collective-permute-done.5
  78.3 0.7 copy-done.15
  79.0 0.2 fusion.14
  79.2 0.2 convolution_add_fusion.8
  79.5 2.9 %collective-permute-start.8 = (f32[12,128]{1,0:T(8,128)S(1)}, f32[12,128]{1,0:T(8,128)S(1)}, u32[]{:S(2)}, u32[]{:S(2)}) collective-permute-start(f32[12,128]{1,0:T(8,128)S(1)} %get-tuple-element.16), channel_id=1, source_target_pairs={{0,24},{8,16},{16,8},{24,0},{1,25},{9,17},{17,9},{25,1},{2,26},{10... | collective-permute-start | bytes 18440 | tf_op jit(solution)/shard_map/ppermute | solution.py:19
  82.4 2.4 %collective-permute-start.7 = (f32[12,128]{1,0:T(8,128)S(1)}, f32[12,128]{1,0:T(8,128)S(1)}, u32[]{:S(2)}, u32[]{:S(2)}) collective-permute-start(f32[12,128]{1,0:T(8,128)S(1)} %get-tuple-element.17), channel_id=1, source_target_pairs={{0,16},{8,24},{16,0},{24,8},{1,17},{9,25},{17,1},{25,9},{2,18},{10... | collective-permute-start | bytes 18440 | tf_op jit(solution)/shard_map/ppermute | solution.py:19
  84.8 3.7 %collective-permute-start.6 = (f32[12,128]{1,0:T(8,128)S(1)}, f32[12,128]{1,0:T(8,128)S(1)}, u32[]{:S(2)}, u32[]{:S(2)}) collective-permute-start(f32[12,128]{1,0:T(8,128)S(1)} %get-tuple-element.18), channel_id=1, source_target_pairs={{0,8},{8,0},{16,24},{24,16},{1,9},{9,1},{17,25},{25,17},{2,10},{10... | collective-permute-start | bytes 18440 | tf_op jit(solution)/shard_map/ppermute | solution.py:19
  88.5 1.9 %fusion.20 = f32[384,128]{1,0:T(8,128)} fusion(f32[384,128]{1,0:T(8,128)} %copy-done.8, f32[256,128]{1,0:T(8,128)} %copy-done.14), kind=kOutput, calls=%fused_computation.38 | convolution fusion | flops 75497472 | bytes 458752 | tf_op jit(solution)/shard_map/dot_general | solution.py:36
  90.4 2.5 %shard_map.59 = (f32[16,12,128]{2,1,0:T(8,128)}, f32[12,128]{1,0:T(8,128)S(1)}, f32[4,12,128]{2,1,0:T(8,128)S(1)}) custom-call(f32[12,128]{1,0:T(8,128)S(1)} %get-tuple-element.19.refs_0_, f32[12,128]{1,0:T(8,128)S(1)} %collective-permute-done.6.refs_1_, f32[12,128]{1,0:T(8,128)S(1)} %collective-permute-done.7.refs_2_, ...), custom_call_target="tpu_custom_call" | custom-call | flops 40000000 | bytes 3000000 | tf_op jit(solution)/shard_map/pallas_call | solution.py:205
  92.9 7.1 %all-to-all-start.3 = ((f32[16,12,128]{2,1,0:T(8,128)}), f32[16,12,128]{2,1,0:T(8,128)S(1)}, u32[]{:S(2)}, u32[]{:S(2)}) async-start(f32[16,12,128]{2,1,0:T(8,128)} %get-tuple-element.5), calls=%async_computation.3 | async-start | bytes 262144 | tf_op jit(solution)/shard_map/all_to_all | solution.py:23
  100.1 0.0 copy-start.16
  100.1 2.0 %convolution_add_fusion.4 = f32[384,128]{1,0:T(8,128)} fusion(f32[384,128]{1,0:T(8,128)} %fusion.20, f32[384,128]{1,0:T(8,128)S(1)} %convolution_add_fusion.5, f32[256,128]{1,0:T(8,128)S(1)} %get-tuple-element.10), kind=kOutput, calls=%fused_computation.7 | convolution fusion | flops 75546624 | bytes 655360 | tf_op jit(solution)/shard_map/dot_general | solution.py:36
  102.1 0.3 fusion.16
  102.4 9.6 %all-to-all-done.3.got_ref = f32[16,12,128]{2,1,0:T(8,128)S(1)} async-done(((f32[16,12,128]{2,1,0:T(8,128)}), f32[16,12,128]{2,1,0:T(8,128)S(1)}, u32[]{:S(2)}, u32[]{:S(2)}) %all-to-all-start.3) | async-done | bytes 98336 | tf_op jit(solution)/shard_map/all_to_all | solution.py:23
  112.0 3.8 %shard_map.60 = f32[32,12,128]{2,1,0:T(8,128)} custom-call(f32[16,12,128]{2,1,0:T(8,128)S(1)} %all-to-all-done.3.got_ref, f32[12,128]{1,0:T(8,128)S(1)} %get-tuple-element.6.own_ref, f32[4,12,128]{2,1,0:T(8,128)S(1)} %get-tuple-element.7.middle_ref, f32[16,8,8,256]{3,2,1,0:T(8,128)S(1)} %all-to-all-done.2.refs_4_.mine_ref, ...), custom_call_target="tpu_custom_call" | custom-call | flops 40000000 | bytes 3000000 | tf_op jit(solution)/shard_map/pallas_call | solution.py:219
  115.9 7.8 %all-to-all-start.4 = ((f32[32,12,128]{2,1,0:T(8,128)}), f32[32,12,128]{2,1,0:T(8,128)S(1)}, u32[]{:S(2)}, u32[]{:S(2)}) async-start(f32[32,12,128]{2,1,0:T(8,128)} %shard_map.60), calls=%async_computation.4 | async-start | bytes 524288 | tf_op jit(solution)/shard_map/all_to_all | solution.py:23
  123.7 0.3 convolution_add_fusion.1
  124.0 8.0 %all-to-all-done.4 = f32[32,12,128]{2,1,0:T(8,128)S(1)} async-done(((f32[32,12,128]{2,1,0:T(8,128)}), f32[32,12,128]{2,1,0:T(8,128)S(1)}, u32[]{:S(2)}, u32[]{:S(2)}) %all-to-all-start.4) | async-done | bytes 196640 | tf_op jit(solution)/shard_map/all_to_all | solution.py:23
  132.1 0.3 fusion.26
  132.4 0.3 convolution_add_fusion
  132.7 0.3 fusion.31
  133.0 0.6 copy-done.11
  133.6 0.3 convolution_add_fusion.3
  134.0 0.4 fusion.36
  134.4 0.5 copy-done.10
  134.9 0.4 convolution_add_fusion.6
  135.3 0.5 copy-done.5
  135.8 0.1 copy-done.9
  135.9 0.8 fusion.2
  136.7 0.0 copy-start.3
  136.7 0.6 fusion.1
  137.3 0.1 copy-done.3
  137.4 11.3 %all_to_all.35 = f32[32,3,128]{2,1,0:T(4,128)S(1)} all-to-all(f32[32,3,128]{2,1,0:T(4,128)S(1)} %broadcast_in_dim.30), channel_id=1, replica_groups=mesh['z'=16,'x'=4,'c'=2,'y'=4] {'x','c','y'}, dimensions={0} | all-to-all | bytes 98304 | tf_op jit(solution)/shard_map/all_to_all | solution.py:23
  148.8 14.7 %all_to_all.36 = f32[16,3,128]{2,1,0:T(4,128)S(1)} all-to-all(f32[16,3,128]{2,1,0:T(4,128)S(1)} %broadcast_in_dim.31), channel_id=1, replica_groups=mesh['z'=16,'x'=4,'c'=2,'y'=4] {'z'}, dimensions={0} | all-to-all | bytes 49152 | tf_op jit(solution)/shard_map/all_to_all | solution.py:23
  163.5 0.6 sqrt_bitcast_fusion
  (50 shorter events, 0.3 us)
Async XLA Ops:
  0.6 136.1 %copy-start = (f32[1,256,256]{2,1,0:T(8,128)S(1)}, f32[1,256,256]{2,1,0:T(8,128)}, u32[]{:S(2)}) copy-start(f32[1,256,256]{2,1,0:T(8,128)} %param.6) | copy-start | bytes 786436
  0.6 10.6 %copy-start.1 = (f32[384,256]{1,0:T(8,128)S(1)}, f32[384,256]{1,0:T(8,128)}, u32[]{:S(2)}) copy-start(f32[384,256]{1,0:T(8,128)} %param.4) | copy-start | bytes 1179652
  0.7 19.6 %all-to-all-start = ((f32[32,8,256]{2,1,0:T(8,128)}), f32[32,8,256]{2,1,0:T(8,128)S(1)}, u32[]{:S(2)}, u32[]{:S(2)}) async-start(f32[32,8,256]{2,1,0:T(8,128)} %bitcast.47), calls=%async_computation | async-start | bytes 524288 | tf_op jit(solution)/shard_map/all_to_all | solution.py:23
  11.3 4.7 %copy-start.2 = (f32[1,256,256]{2,1,0:T(8,128)S(1)}, f32[1,256,256]{2,1,0:T(8,128)}, u32[]{:S(2)}) copy-start(f32[1,256,256]{2,1,0:T(8,128)} %param.7) | copy-start | bytes 786436
  12.7 21.3 %collective-permute-start.1 = (f32[384,128]{1,0:T(8,128)S(1)}, f32[384,128]{1,0:T(8,128)S(1)}, u32[]{:S(2)}, u32[]{:S(2)}) collective-permute-start(f32[384,128]{1,0:T(8,128)S(1)} %fusion.8), channel_id=1, source_target_pairs={{0,1},{1,0},{2,3},{3,2},{4,5},{5,4},{6,7},{7,6},{8,9},{9,8},{10,11... | collective-permute-start | bytes 589832 | tf_op jit(solution)/shard_map/ppermute | solution.py:19
  16.0 17.9 %collective-permute-start = (f32[256,256]{1,0:T(8,128)S(1)}, f32[256,256]{1,0:T(8,128)S(1)}, u32[]{:S(2)}, u32[]{:S(2)}) collective-permute-start(f32[256,256]{1,0:T(8,128)S(1)} %bitcast.48), channel_id=1, source_target_pairs={{0,1},{1,0},{2,3},{3,2},{4,5},{5,4},{6,7},{7,6},{8,9},{9,8},{10,11... | collective-permute-start | bytes 786440 | tf_op jit(solution)/shard_map/ppermute | solution.py:19
  18.1 1.0 copy-start.4
  20.9 25.0 %all-to-all-start.1 = ((f32[16,8,256]{2,1,0:T(8,128)}), f32[16,8,256]{2,1,0:T(8,128)S(1)}, u32[]{:S(2)}, u32[]{:S(2)}) async-start(f32[16,8,256]{2,1,0:T(8,128)} %broadcast_in_dim.13), calls=%async_computation.1 | async-start | bytes 262144 | tf_op jit(solution)/shard_map/all_to_all | solution.py:23
  34.7 27.1 %collective-permute-start.3 = (f32[384,128]{1,0:T(8,128)S(1)}, f32[384,128]{1,0:T(8,128)S(1)}, u32[]{:S(2)}, u32[]{:S(2)}) collective-permute-start(f32[384,128]{1,0:T(8,128)S(1)} %convolution_add_fusion.5), channel_id=1, source_target_pairs={{0,2},{1,3},{2,0},{3,1},{4,6},{5,7},{6,4},{7,5},{8,10},{9,11},{10,... | collective-permute-start | bytes 589832 | tf_op jit(solution)/shard_map/ppermute | solution.py:19
  39.5 15.6 %collective-permute-start.2 = (f32[256,256]{1,0:T(8,128)S(1)}, f32[256,256]{1,0:T(8,128)S(1)}, u32[]{:S(2)}, u32[]{:S(2)}) collective-permute-start(f32[256,256]{1,0:T(8,128)S(1)} %broadcast_select_fusion.1), channel_id=1, source_target_pairs={{0,2},{1,3},{2,0},{3,1},{4,6},{5,7},{6,4},{7,5},{8,10},{9,11},{10,... | collective-permute-start | bytes 786440 | tf_op jit(solution)/shard_map/ppermute | solution.py:19
  47.0 19.0 %all-to-all-start.2 = ((f32[16,8,8,256]{3,2,1,0:T(8,128)}), f32[16,8,8,256]{3,2,1,0:T(8,128)S(1)}, u32[]{:S(2)}, u32[]{:S(2)}) async-start(f32[16,8,8,256]{3,2,1,0:T(8,128)} %broadcast_in_dim.28), calls=%async_computation.2 | async-start | bytes 2097152 | tf_op jit(solution)/shard_map/all_to_all | solution.py:23
  55.8 21.1 %collective-permute-start.4 = (f32[256,256]{1,0:T(8,128)}, f32[256,256]{1,0:T(8,128)}, u32[]{:S(2)}, u32[]{:S(2)}) collective-permute-start(f32[256,256]{1,0:T(8,128)} %broadcast_select_fusion), channel_id=1, source_target_pairs={{0,4},{4,0},{1,5},{5,1},{2,6},{6,2},{3,7},{7,3},{8,12},{12,8},{9,1... | collective-permute-start | bytes 786440 | tf_op jit(solution)/shard_map/ppermute | solution.py:19
  61.7 1.0 copy-start.14
  61.8 1.0 copy-start.8
  66.0 24.4 %collective-permute-start.9 = (f32[16,8,8,256]{3,2,1,0:T(8,128)S(1)}, f32[16,8,8,256]{3,2,1,0:T(8,128)S(1)}, u32[]{:S(2)}, u32[]{:S(2)}) collective-permute-start(f32[16,8,8,256]{3,2,1,0:T(8,128)S(1)} %all-to-all-done.2.refs_4_.mine_ref), channel_id=1, source_target_pairs={{0,4},{4,0},{1,5},{5,1},{2,6},{6,2},{3,7},{7,3},{8,12},{12,8},{9,1... | collective-permute-start | bytes 3145736 | tf_op jit(solution)/shard_map/ppermute | solution.py:19
  74.9 4.3 %copy-start.6 = (f32[384,128]{1,0:T(8,128)}, f32[384,128]{1,0:T(8,128)S(1)}, u32[]{:S(2)}) copy-start(f32[384,128]{1,0:T(8,128)S(1)} %convolution_add_fusion.2) | copy-start | bytes 589828
  75.0 3.3 %collective-permute-start.5 = (f32[384,128]{1,0:T(8,128)S(1)}, f32[384,128]{1,0:T(8,128)S(1)}, u32[]{:S(2)}, u32[]{:S(2)}) collective-permute-start(f32[384,128]{1,0:T(8,128)S(1)} %convolution_add_fusion.2), channel_id=1, source_target_pairs={{0,4},{4,0},{1,5},{5,1},{2,6},{6,2},{3,7},{7,3},{8,12},{12,8},{9,1... | collective-permute-start | bytes 589832 | tf_op jit(solution)/shard_map/ppermute | solution.py:19
  78.0 1.4 copy-start.12
  78.3 0.7 copy-start.15
  79.5 10.9 %collective-permute-start.8 = (f32[12,128]{1,0:T(8,128)S(1)}, f32[12,128]{1,0:T(8,128)S(1)}, u32[]{:S(2)}, u32[]{:S(2)}) collective-permute-start(f32[12,128]{1,0:T(8,128)S(1)} %get-tuple-element.16), channel_id=1, source_target_pairs={{0,24},{8,16},{16,8},{24,0},{1,25},{9,17},{17,9},{25,1},{2,26},{10... | collective-permute-start | bytes 18440 | tf_op jit(solution)/shard_map/ppermute | solution.py:19
  82.4 8.0 %collective-permute-start.7 = (f32[12,128]{1,0:T(8,128)S(1)}, f32[12,128]{1,0:T(8,128)S(1)}, u32[]{:S(2)}, u32[]{:S(2)}) collective-permute-start(f32[12,128]{1,0:T(8,128)S(1)} %get-tuple-element.17), channel_id=1, source_target_pairs={{0,16},{8,24},{16,0},{24,8},{1,17},{9,25},{17,1},{25,9},{2,18},{10... | collective-permute-start | bytes 18440 | tf_op jit(solution)/shard_map/ppermute | solution.py:19
  84.8 5.6 %collective-permute-start.6 = (f32[12,128]{1,0:T(8,128)S(1)}, f32[12,128]{1,0:T(8,128)S(1)}, u32[]{:S(2)}, u32[]{:S(2)}) collective-permute-start(f32[12,128]{1,0:T(8,128)S(1)} %get-tuple-element.18), channel_id=1, source_target_pairs={{0,8},{8,0},{16,24},{24,16},{1,9},{9,1},{17,25},{25,17},{2,10},{10... | collective-permute-start | bytes 18440 | tf_op jit(solution)/shard_map/ppermute | solution.py:19
  92.9 19.1 %all-to-all-start.3 = ((f32[16,12,128]{2,1,0:T(8,128)}), f32[16,12,128]{2,1,0:T(8,128)S(1)}, u32[]{:S(2)}, u32[]{:S(2)}) async-start(f32[16,12,128]{2,1,0:T(8,128)} %get-tuple-element.5), calls=%async_computation.3 | async-start | bytes 262144 | tf_op jit(solution)/shard_map/all_to_all | solution.py:23
  100.1 2.0 %copy-start.13 = (f32[256,128]{1,0:T(8,128)S(1)}, f32[256,128]{1,0:T(8,128)}, u32[]{:S(2)}) copy-start(f32[256,128]{1,0:T(8,128)} %copy-done.12) | copy-start | bytes 393220
  100.1 2.0 %copy-start.16 = (f32[384,128]{1,0:T(8,128)S(1)}, f32[384,128]{1,0:T(8,128)}, u32[]{:S(2)}) copy-start(f32[384,128]{1,0:T(8,128)} %copy-done.15) | copy-start | bytes 589828
  115.9 7.8 %copy-start.7 = (f32[384,128]{1,0:T(8,128)S(1)}, f32[384,128]{1,0:T(8,128)}, u32[]{:S(2)}) copy-start(f32[384,128]{1,0:T(8,128)} %copy-done.6) | copy-start | bytes 589828
  115.9 16.2 %all-to-all-start.4 = ((f32[32,12,128]{2,1,0:T(8,128)}), f32[32,12,128]{2,1,0:T(8,128)S(1)}, u32[]{:S(2)}, u32[]{:S(2)}) async-start(f32[32,12,128]{2,1,0:T(8,128)} %shard_map.60), calls=%async_computation.4 | async-start | bytes 524288 | tf_op jit(solution)/shard_map/all_to_all | solution.py:23
  132.7 0.9 copy-start.11
  133.9 0.9 copy-start.10
  134.9 0.9 copy-start.5
  134.9 1.0 copy-start.9
  136.7 0.7 copy-start.3

commit v4 on v3

--- a/solution.py
+++ b/solution.py
@@ -189,11 +189,22 @@
         theirs = jnp.where(is_left, other_chain[:, half:], chain[:, :half])
         chain = jnp.where(is_left, chain, other_chain)
         eliminated = apply_block(skeleton, mine[:half]) + apply_block(other, theirs[:half])
+        part = apply_transpose(eliminated, mine[:half])
         if (axis, bit) == hops[-1]:
             skeleton = lax.dynamic_slice_in_dim(skeleton, first, stretch, 0)
             other = lax.dynamic_slice_in_dim(other, first, stretch, 0)
         skeleton = apply_block(skeleton, mine[half:]) + apply_block(other, theirs[half:])
-        lower.append((mine, eliminated))
+        lower.append((mine[half:], part))
+
+    through = lower[-1][0]
+    for block, _ in reversed(lower[:-1]):
+        through = apply_transpose(through, block)
+    through = apply_transpose(through, leaf_block[half:])
+    rest = lower[-1][1]
+    for block, part in reversed(lower[:-1]):
+        rest = part + apply_transpose(rest, block)
+    rest = apply_transpose(rest, leaf_block[half:])
+    rest = rest + apply_transpose(leaf_part, leaf_block[:half])
 
     shares = skeleton.reshape(groups, share, half)
     own = [lax.dynamic_index_in_dim(shares, x, 0, False)]
@@ -225,9 +236,7 @@
         compiler_params=pltpu.CompilerParams(vmem_limit_bytes=LIMIT),
     )(got, own, middle, *blocks)
     known = direct(known, ("c", "y", "x")).reshape(rhs, half)
-    for mine, eliminated in reversed(lower):
-        known = apply_transpose(eliminated, mine[:half]) + apply_transpose(known, mine[half:])
-    solved = apply_transpose(jnp.concatenate([leaf_part, known], axis=1), leaf_block)
+    solved = rest + apply_transpose(known, through)
     residual = right_side - apply_block(solved, leaf_diag[0])
     squares = jnp.sum(residual * residual, axis=1).reshape(-1, 128)
     totals = jnp.sum(to_each(squares, PLANE), axis=0)

time: 165 us -> 165 us (level)
  waiting for transfers between devices: 25.5 us -> 28.7 us
  starting transfers between devices: 81.8 us -> 79.9 us
  other arithmetic: 2.62 us -> 0.84 us
    ppermute x10, waiting for transfers between devices: 0.27 us -> 6.37 us  [swapped(): return lax.ppermute(block, axis, [(i, i ^ bit) for i in range(count)])]
    dot_general x15, matrix products: 12.5 us -> 8.33 us  [apply_block(): lax.dot_general(vectors, block, (((1,), (1,)), ((), ())), precision=PRECI...]
    dot_general x7 -> x11, matrix products: 2.85 us -> 6.9 us  [apply_transpose(): jnp.dot(vectors, block, precision=PRECISE, preferred_element_type=jnp.flo...]
    ppermute x10, starting transfers between devices: 36.5 us -> 32.9 us  [swapped(): return lax.ppermute(block, axis, [(i, i ^ bit) for i in range(count)])]
    all_to_all x5, waiting for transfers between devices: 25.3 us -> 22.3 us  [direct(): return lax.all_to_all(parts, axes, 0, 0)]
    all_to_all x5, starting transfers between devices: 45.3 us -> 47 us  [direct(): return lax.all_to_all(parts, axes, 0, 0)]
    unnamed x41 -> x25, local copies, waits for them, and re-layouts: 3.44 us -> 2.23 us
  transfers between devices with their start and end apart: 15 -> 15, of which waited for: 5 -> 4; matrix products, arithmetic and copies ran while one was open for 10% -> 10% of each run, Pallas kernels for 0% -> 0%
where the time goes in v4:
time: 165 us; the launch traced here: 164 us
  starting transfers between devices  79.9 us (48%)
  waiting for transfers between devices  28.7 us (17%)
  blocking collectives  27.5 us (17%)
  matrix products  15.2 us (9%)
  Pallas kernels  6.31 us (4%)
  local copies, waits for them, and re-layouts  4.08 us (2%)
    all_to_all x5, starting transfers between devices, direct(): return lax.all_to_all(parts, axes, 0, 0)  47 us
    ppermute x10, starting transfers between devices, swapped(): return lax.ppermute(block, axis, [(i, i ^ bit) for i in range(count)])  32.9 us
    all_to_all x2, blocking collectives, direct(): return lax.all_to_all(parts, axes, 0, 0)  27.5 us
    all_to_all x5, waiting for transfers between devices, direct(): return lax.all_to_all(parts, axes, 0, 0)  22.3 us
    dot_general x15, matrix products, apply_block(): lax.dot_general(vectors, block, (((1,), (1,)), ((), ())), precision=PRECI...  8.33 us
    dot_general x11, matrix products, apply_transpose(): jnp.dot(vectors, block, precision=PRECISE, preferred_element_type=jnp.flo...  6.9 us
    ppermute x10, waiting for transfers between devices, swapped(): return lax.ppermute(block, axis, [(i, i ^ bit) for i in range(count)])  6.37 us
    pallas_call x1, Pallas kernels, body(): pl.pallas_call(kernel, out_shape=jax.ShapeDtypeStruct((members, share, ha...  3.84 us
  transfers between devices with their start and end apart: 15, of which 4 were waited for; matrix products, arithmetic and copies ran while one was open for 10% of the time, Pallas kernels for 0%

profile of v4, /device:TPU:1, one launch (start us, length us, event | category | flops | bytes accessed | tf_op | source)
XLA Modules:
  0.0 163.7 jit_solution(3168477760317593410)
XLA Ops:
  0.6 0.0 copy-start
  0.7 10.6 %all-to-all-start = ((f32[32,8,256]{2,1,0:T(8,128)}), f32[32,8,256]{2,1,0:T(8,128)S(1)}, u32[]{:S(2)}, u32[]{:S(2)}) async-start(f32[32,8,256]{2,1,0:T(8,128)} %bitcast.55), calls=%async_computation | async-start | bytes 524288 | tf_op jit(solution)/shard_map/all_to_all | solution.py:23
  11.3 0.0 copy-start.2
  11.3 1.4 fusion.10
  12.7 3.3 %collective-permute-start.1 = (f32[384,128]{1,0:T(8,128)S(1)}, f32[384,128]{1,0:T(8,128)S(1)}, u32[]{:S(2)}, u32[]{:S(2)}) collective-permute-start(f32[384,128]{1,0:T(8,128)S(1)} %fusion.10), channel_id=1, source_target_pairs={{0,1},{1,0},{2,3},{3,2},{4,5},{5,4},{6,7},{7,6},{8,9},{9,8},{10,11... | collective-permute-start | bytes 589832 | tf_op jit(solution)/shard_map/ppermute | solution.py:19
  16.0 2.0 %collective-permute-start = (f32[256,256]{1,0:T(8,128)S(1)}, f32[256,256]{1,0:T(8,128)S(1)}, u32[]{:S(2)}, u32[]{:S(2)}) collective-permute-start(f32[256,256]{1,0:T(8,128)S(1)} %bitcast.56), channel_id=1, source_target_pairs={{0,1},{1,0},{2,3},{3,2},{4,5},{5,4},{6,7},{7,6},{8,9},{9,8},{10,11... | collective-permute-start | bytes 786440 | tf_op jit(solution)/shard_map/ppermute | solution.py:19
  18.1 0.0 copy-start.3
  18.1 0.9 copy.9
  19.0 0.0 copy-done.3
  19.0 1.2 fusion.4
  20.2 0.7 broadcast_in_dim.13
  20.9 13.0 %all-to-all-start.1 = ((f32[16,8,256]{2,1,0:T(8,128)}), f32[16,8,256]{2,1,0:T(8,128)S(1)}, u32[]{:S(2)}, u32[]{:S(2)}) async-start(f32[16,8,256]{2,1,0:T(8,128)} %broadcast_in_dim.13), calls=%async_computation.1 | async-start | bytes 262144 | tf_op jit(solution)/shard_map/all_to_all | solution.py:23
  33.9 0.0 collective-permute-done
  34.0 0.0 collective-permute-done.1
  34.0 0.3 fusion.25
  34.3 0.3 convolution_add_fusion.6
  34.6 4.8 %collective-permute-start.3 = (f32[384,128]{1,0:T(8,128)S(1)}, f32[384,128]{1,0:T(8,128)S(1)}, u32[]{:S(2)}, u32[]{:S(2)}) collective-permute-start(f32[384,128]{1,0:T(8,128)S(1)} %convolution_add_fusion.6), channel_id=1, source_target_pairs={{0,2},{1,3},{2,0},{3,1},{4,6},{5,7},{6,4},{7,5},{8,10},{9,11},{10,... | collective-permute-start | bytes 589832 | tf_op jit(solution)/shard_map/ppermute | solution.py:19
  39.5 2.0 %collective-permute-start.2 = (f32[256,256]{1,0:T(8,128)S(1)}, f32[256,256]{1,0:T(8,128)S(1)}, u32[]{:S(2)}, u32[]{:S(2)}) collective-permute-start(f32[256,256]{1,0:T(8,128)S(1)} %broadcast_select_fusion.1), channel_id=1, source_target_pairs={{0,2},{1,3},{2,0},{3,1},{4,6},{5,7},{6,4},{7,5},{8,10},{9,11},{10,... | collective-permute-start | bytes 786440 | tf_op jit(solution)/shard_map/ppermute | solution.py:19
  41.5 0.3 fusion.27
  41.8 1.0 convolution_add_fusion.8
  42.9 6.3 %collective-permute-done.2 = f32[256,256]{1,0:T(8,128)S(1)} collective-permute-done((f32[256,256]{1,0:T(8,128)S(1)}, f32[256,256]{1,0:T(8,128)S(1)}, u32[]{:S(2)}, u32[]{:S(2)}) %collective-permute-start.2) | collective-permute-done | bytes 262176 | tf_op jit(solution)/shard_map/ppermute | solution.py:19
  49.2 0.0 collective-permute-done.3
  49.3 0.3 fusion.21
  49.6 0.3 convolution_add_fusion.3
  49.9 4.3 %collective-permute-start.5 = (f32[384,128]{1,0:T(8,128)S(1)}, f32[384,128]{1,0:T(8,128)S(1)}, u32[]{:S(2)}, u32[]{:S(2)}) collective-permute-start(f32[384,128]{1,0:T(8,128)S(1)} %convolution_add_fusion.3), channel_id=1, source_target_pairs={{0,4},{4,0},{1,5},{5,1},{2,6},{6,2},{3,7},{7,3},{8,12},{12,8},{9,1... | collective-permute-start | bytes 589832 | tf_op jit(solution)/shard_map/ppermute | solution.py:19
  54.3 1.9 %collective-permute-start.4 = (f32[256,256]{1,0:T(8,128)S(1)}, f32[256,256]{1,0:T(8,128)S(1)}, u32[]{:S(2)}, u32[]{:S(2)}) collective-permute-start(f32[256,256]{1,0:T(8,128)S(1)} %broadcast_select_fusion), channel_id=1, source_target_pairs={{0,4},{4,0},{1,5},{5,1},{2,6},{6,2},{3,7},{7,3},{8,12},{12,8},{9,1... | collective-permute-start | bytes 786440 | tf_op jit(solution)/shard_map/ppermute | solution.py:19
  56.2 0.3 fusion.23
  56.5 1.0 convolution_add_fusion.5
  57.6 1.1 broadcast_in_dim.28
  58.7 6.1 %all-to-all-start.2 = ((f32[16,8,8,256]{3,2,1,0:T(8,128)}), f32[16,8,8,256]{3,2,1,0:T(8,128)S(1)}, u32[]{:S(2)}, u32[]{:S(2)}) async-start(f32[16,8,8,256]{3,2,1,0:T(8,128)} %broadcast_in_dim.28), calls=%async_computation.2 | async-start | bytes 2097152 | tf_op jit(solution)/shard_map/all_to_all | solution.py:23
  64.8 0.0 collective-permute-done.5
  64.8 0.2 fusion.17
  65.1 0.2 convolution_add_fusion.9
  65.4 3.3 %collective-permute-start.6 = (f32[12,128]{1,0:T(8,128)S(1)}, f32[12,128]{1,0:T(8,128)S(1)}, u32[]{:S(2)}, u32[]{:S(2)}) collective-permute-start(f32[12,128]{1,0:T(8,128)S(1)} %get-tuple-element.18), channel_id=1, source_target_pairs={{0,8},{8,0},{16,24},{24,16},{1,9},{9,1},{17,25},{25,17},{2,10},{10... | collective-permute-start | bytes 18440 | tf_op jit(solution)/shard_map/ppermute | solution.py:19
  68.6 4.3 %collective-permute-start.7 = (f32[12,128]{1,0:T(8,128)S(1)}, f32[12,128]{1,0:T(8,128)S(1)}, u32[]{:S(2)}, u32[]{:S(2)}) collective-permute-start(f32[12,128]{1,0:T(8,128)S(1)} %get-tuple-element.17), channel_id=1, source_target_pairs={{0,16},{8,24},{16,0},{24,8},{1,17},{9,25},{17,1},{25,9},{2,18},{10... | collective-permute-start | bytes 18440 | tf_op jit(solution)/shard_map/ppermute | solution.py:19
  72.9 2.0 %collective-permute-start.8 = (f32[12,128]{1,0:T(8,128)S(1)}, f32[12,128]{1,0:T(8,128)S(1)}, u32[]{:S(2)}, u32[]{:S(2)}) collective-permute-start(f32[12,128]{1,0:T(8,128)S(1)} %get-tuple-element.16), channel_id=1, source_target_pairs={{0,24},{8,16},{16,8},{24,0},{1,25},{9,17},{17,9},{25,1},{2,26},{10... | collective-permute-start | bytes 18440 | tf_op jit(solution)/shard_map/ppermute | solution.py:19
  75.0 0.3 fusion.19
  75.3 0.3 convolution_add_fusion.2
  75.6 0.3 fusion.32
  76.0 0.3 fusion.40
  76.3 4.1 %all-to-all-done.2.refs_4_.mine_ref = f32[16,8,8,256]{3,2,1,0:T(8,128)S(1)} async-done(((f32[16,8,8,256]{3,2,1,0:T(8,128)}), f32[16,8,8,256]{3,2,1,0:T(8,128)S(1)}, u32[]{:S(2)}, u32[]{:S(2)}) %all-to-all-start.2) | async-done | bytes 1048608 | tf_op jit(solution)/shard_map/all_to_all | solution.py:23
  80.4 5.1 %collective-permute-start.9 = (f32[16,8,8,256]{3,2,1,0:T(8,128)S(1)}, f32[16,8,8,256]{3,2,1,0:T(8,128)S(1)}, u32[]{:S(2)}, u32[]{:S(2)}) collective-permute-start(f32[16,8,8,256]{3,2,1,0:T(8,128)S(1)} %all-to-all-done.2.refs_4_.mine_ref), channel_id=1, source_target_pairs={{0,4},{4,0},{1,5},{5,1},{2,6},{6,2},{3,7},{7,3},{8,12},{12,8},{9,1... | collective-permute-start | bytes 3145736 | tf_op jit(solution)/shard_map/ppermute | solution.py:19
  85.5 1.2 convolution_add_fusion.4
  86.7 0.3 fusion.45
  87.0 0.6 copy-done.6
  87.6 0.3 convolution_add_fusion.7
  87.9 1.2 fusion.8
  89.2 0.2 fusion.29
  89.4 2.5 %shard_map.59 = (f32[16,12,128]{2,1,0:T(8,128)}, f32[12,128]{1,0:T(8,128)S(1)}, f32[4,12,128]{2,1,0:T(8,128)S(1)}) custom-call(f32[12,128]{1,0:T(8,128)S(1)} %get-tuple-element.19.refs_0_, f32[12,128]{1,0:T(8,128)S(1)} %collective-permute-done.6.refs_1_, f32[12,128]{1,0:T(8,128)S(1)} %collective-permute-done.7.refs_2_, ...), custom_call_target="tpu_custom_call" | custom-call | flops 40000000 | bytes 3000000 | tf_op jit(solution)/shard_map/pallas_call | solution.py:216
  91.9 11.6 %all-to-all-start.3 = ((f32[16,12,128]{2,1,0:T(8,128)}), f32[16,12,128]{2,1,0:T(8,128)S(1)}, u32[]{:S(2)}, u32[]{:S(2)}) async-start(f32[16,12,128]{2,1,0:T(8,128)} %get-tuple-element.5), calls=%async_computation.3 | async-start | bytes 262144 | tf_op jit(solution)/shard_map/all_to_all | solution.py:23
  103.5 0.8 fusion.43
  104.3 1.5 convolution_add_fusion.1
  105.8 10.1 %all-to-all-done.3.got_ref = f32[16,12,128]{2,1,0:T(8,128)S(1)} async-done(((f32[16,12,128]{2,1,0:T(8,128)}), f32[16,12,128]{2,1,0:T(8,128)S(1)}, u32[]{:S(2)}, u32[]{:S(2)}) %all-to-all-start.3) | async-done | bytes 98336 | tf_op jit(solution)/shard_map/all_to_all | solution.py:23
  115.9 3.8 %shard_map.60 = f32[32,12,128]{2,1,0:T(8,128)} custom-call(f32[16,12,128]{2,1,0:T(8,128)S(1)} %all-to-all-done.3.got_ref, f32[12,128]{1,0:T(8,128)S(1)} %get-tuple-element.6.own_ref, f32[4,12,128]{2,1,0:T(8,128)S(1)} %get-tuple-element.7.middle_ref, f32[16,8,8,256]{3,2,1,0:T(8,128)S(1)} %all-to-all-done.2.refs_4_.mine_ref, ...), custom_call_target="tpu_custom_call" | custom-call | flops 40000000 | bytes 3000000 | tf_op jit(solution)/shard_map/pallas_call | solution.py:230
  119.8 5.7 %all-to-all-start.4 = ((f32[32,12,128]{2,1,0:T(8,128)}), f32[32,12,128]{2,1,0:T(8,128)S(1)}, u32[]{:S(2)}, u32[]{:S(2)}) async-start(f32[32,12,128]{2,1,0:T(8,128)} %shard_map.60), calls=%async_computation.4 | async-start | bytes 524288 | tf_op jit(solution)/shard_map/all_to_all | solution.py:23
  125.5 0.3 fusion.6
  125.7 8.1 %all-to-all-done.4 = f32[32,12,128]{2,1,0:T(8,128)S(1)} async-done(((f32[32,12,128]{2,1,0:T(8,128)}), f32[32,12,128]{2,1,0:T(8,128)S(1)}, u32[]{:S(2)}, u32[]{:S(2)}) %all-to-all-start.4) | async-done | bytes 196640 | tf_op jit(solution)/shard_map/all_to_all | solution.py:23
  133.8 0.5 convolution_add_fusion
  134.3 0.5 copy-done.4
  134.8 0.6 fusion.1
  135.4 0.1 copy-done.5
  135.5 11.3 %all_to_all.35 = f32[32,3,128]{2,1,0:T(4,128)S(1)} all-to-all(f32[32,3,128]{2,1,0:T(4,128)S(1)} %broadcast_in_dim.30), channel_id=1, replica_groups=mesh['z'=16,'x'=4,'c'=2,'y'=4] {'x','c','y'}, dimensions={0} | all-to-all | bytes 98304 | tf_op jit(solution)/shard_map/all_to_all | solution.py:23
  146.9 16.1 %all_to_all.36 = f32[16,3,128]{2,1,0:T(4,128)S(1)} all-to-all(f32[16,3,128]{2,1,0:T(4,128)S(1)} %broadcast_in_dim.31), channel_id=1, replica_groups=mesh['z'=16,'x'=4,'c'=2,'y'=4] {'z'}, dimensions={0} | all-to-all | bytes 49152 | tf_op jit(solution)/shard_map/all_to_all | solution.py:23
  163.1 0.6 sqrt_bitcast_fusion
  (38 shorter events, 0.4 us)
Async XLA Ops:
  0.6 133.6 %copy-start = (f32[1,256,256]{2,1,0:T(8,128)S(1)}, f32[1,256,256]{2,1,0:T(8,128)}, u32[]{:S(2)}) copy-start(f32[1,256,256]{2,1,0:T(8,128)} %param.6) | copy-start | bytes 786436
  0.6 10.6 %copy-start.1 = (f32[384,256]{1,0:T(8,128)S(1)}, f32[384,256]{1,0:T(8,128)}, u32[]{:S(2)}) copy-start(f32[384,256]{1,0:T(8,128)} %param.4) | copy-start | bytes 1179652
  0.7 19.5 %all-to-all-start = ((f32[32,8,256]{2,1,0:T(8,128)}), f32[32,8,256]{2,1,0:T(8,128)S(1)}, u32[]{:S(2)}, u32[]{:S(2)}) async-start(f32[32,8,256]{2,1,0:T(8,128)} %bitcast.55), calls=%async_computation | async-start | bytes 524288 | tf_op jit(solution)/shard_map/all_to_all | solution.py:23
  11.3 4.7 %copy-start.2 = (f32[1,256,256]{2,1,0:T(8,128)S(1)}, f32[1,256,256]{2,1,0:T(8,128)}, u32[]{:S(2)}) copy-start(f32[1,256,256]{2,1,0:T(8,128)} %param.7) | copy-start | bytes 786436
  12.7 21.2 %collective-permute-start.1 = (f32[384,128]{1,0:T(8,128)S(1)}, f32[384,128]{1,0:T(8,128)S(1)}, u32[]{:S(2)}, u32[]{:S(2)}) collective-permute-start(f32[384,128]{1,0:T(8,128)S(1)} %fusion.10), channel_id=1, source_target_pairs={{0,1},{1,0},{2,3},{3,2},{4,5},{5,4},{6,7},{7,6},{8,9},{9,8},{10,11... | collective-permute-start | bytes 589832 | tf_op jit(solution)/shard_map/ppermute | solution.py:19
  16.0 17.9 %collective-permute-start = (f32[256,256]{1,0:T(8,128)S(1)}, f32[256,256]{1,0:T(8,128)S(1)}, u32[]{:S(2)}, u32[]{:S(2)}) collective-permute-start(f32[256,256]{1,0:T(8,128)S(1)} %bitcast.56), channel_id=1, source_target_pairs={{0,1},{1,0},{2,3},{3,2},{4,5},{5,4},{6,7},{7,6},{8,9},{9,8},{10,11... | collective-permute-start | bytes 786440 | tf_op jit(solution)/shard_map/ppermute | solution.py:19
  18.1 1.0 copy-start.3
  20.9 36.7 %all-to-all-start.1 = ((f32[16,8,256]{2,1,0:T(8,128)}), f32[16,8,256]{2,1,0:T(8,128)S(1)}, u32[]{:S(2)}, u32[]{:S(2)}) async-start(f32[16,8,256]{2,1,0:T(8,128)} %broadcast_in_dim.13), calls=%async_computation.1 | async-start | bytes 262144 | tf_op jit(solution)/shard_map/all_to_all | solution.py:23
  34.6 14.6 %collective-permute-start.3 = (f32[384,128]{1,0:T(8,128)S(1)}, f32[384,128]{1,0:T(8,128)S(1)}, u32[]{:S(2)}, u32[]{:S(2)}) collective-permute-start(f32[384,128]{1,0:T(8,128)S(1)} %convolution_add_fusion.6), channel_id=1, source_target_pairs={{0,2},{1,3},{2,0},{3,1},{4,6},{5,7},{6,4},{7,5},{8,10},{9,11},{10,... | collective-permute-start | bytes 589832 | tf_op jit(solution)/shard_map/ppermute | solution.py:19
  39.5 9.7 %collective-permute-start.2 = (f32[256,256]{1,0:T(8,128)S(1)}, f32[256,256]{1,0:T(8,128)S(1)}, u32[]{:S(2)}, u32[]{:S(2)}) collective-permute-start(f32[256,256]{1,0:T(8,128)S(1)} %broadcast_select_fusion.1), channel_id=1, source_target_pairs={{0,2},{1,3},{2,0},{3,1},{4,6},{5,7},{6,4},{7,5},{8,10},{9,11},{10,... | collective-permute-start | bytes 786440 | tf_op jit(solution)/shard_map/ppermute | solution.py:19
  49.9 14.9 %collective-permute-start.5 = (f32[384,128]{1,0:T(8,128)S(1)}, f32[384,128]{1,0:T(8,128)S(1)}, u32[]{:S(2)}, u32[]{:S(2)}) collective-permute-start(f32[384,128]{1,0:T(8,128)S(1)} %convolution_add_fusion.3), channel_id=1, source_target_pairs={{0,4},{4,0},{1,5},{5,1},{2,6},{6,2},{3,7},{7,3},{8,12},{12,8},{9,1... | collective-permute-start | bytes 589832 | tf_op jit(solution)/shard_map/ppermute | solution.py:19
  54.3 10.5 %collective-permute-start.4 = (f32[256,256]{1,0:T(8,128)S(1)}, f32[256,256]{1,0:T(8,128)S(1)}, u32[]{:S(2)}, u32[]{:S(2)}) collective-permute-start(f32[256,256]{1,0:T(8,128)S(1)} %broadcast_select_fusion), channel_id=1, source_target_pairs={{0,4},{4,0},{1,5},{5,1},{2,6},{6,2},{3,7},{7,3},{8,12},{12,8},{9,1... | collective-permute-start | bytes 786440 | tf_op jit(solution)/shard_map/ppermute | solution.py:19
  58.7 21.7 %all-to-all-start.2 = ((f32[16,8,8,256]{3,2,1,0:T(8,128)}), f32[16,8,8,256]{3,2,1,0:T(8,128)S(1)}, u32[]{:S(2)}, u32[]{:S(2)}) async-start(f32[16,8,8,256]{3,2,1,0:T(8,128)} %broadcast_in_dim.28), calls=%async_computation.2 | async-start | bytes 2097152 | tf_op jit(solution)/shard_map/all_to_all | solution.py:23
  65.4 24.0 %collective-permute-start.6 = (f32[12,128]{1,0:T(8,128)S(1)}, f32[12,128]{1,0:T(8,128)S(1)}, u32[]{:S(2)}, u32[]{:S(2)}) collective-permute-start(f32[12,128]{1,0:T(8,128)S(1)} %get-tuple-element.18), channel_id=1, source_target_pairs={{0,8},{8,0},{16,24},{24,16},{1,9},{9,1},{17,25},{25,17},{2,10},{10... | collective-permute-start | bytes 18440 | tf_op jit(solution)/shard_map/ppermute | solution.py:19
  68.6 20.8 %collective-permute-start.7 = (f32[12,128]{1,0:T(8,128)S(1)}, f32[12,128]{1,0:T(8,128)S(1)}, u32[]{:S(2)}, u32[]{:S(2)}) collective-permute-start(f32[12,128]{1,0:T(8,128)S(1)} %get-tuple-element.17), channel_id=1, source_target_pairs={{0,16},{8,24},{16,0},{24,8},{1,17},{9,25},{17,1},{25,9},{2,18},{10... | collective-permute-start | bytes 18440 | tf_op jit(solution)/shard_map/ppermute | solution.py:19
  72.9 16.4 %collective-permute-start.8 = (f32[12,128]{1,0:T(8,128)S(1)}, f32[12,128]{1,0:T(8,128)S(1)}, u32[]{:S(2)}, u32[]{:S(2)}) collective-permute-start(f32[12,128]{1,0:T(8,128)S(1)} %get-tuple-element.16), channel_id=1, source_target_pairs={{0,24},{8,16},{16,8},{24,0},{1,25},{9,17},{17,9},{25,1},{2,26},{10... | collective-permute-start | bytes 18440 | tf_op jit(solution)/shard_map/ppermute | solution.py:19
  80.4 9.0 %collective-permute-start.9 = (f32[16,8,8,256]{3,2,1,0:T(8,128)S(1)}, f32[16,8,8,256]{3,2,1,0:T(8,128)S(1)}, u32[]{:S(2)}, u32[]{:S(2)}) collective-permute-start(f32[16,8,8,256]{3,2,1,0:T(8,128)S(1)} %all-to-all-done.2.refs_4_.mine_ref), channel_id=1, source_target_pairs={{0,4},{4,0},{1,5},{5,1},{2,6},{6,2},{3,7},{7,3},{8,12},{12,8},{9,1... | collective-permute-start | bytes 3145736 | tf_op jit(solution)/shard_map/ppermute | solution.py:19
  86.7 0.9 copy-start.6
  91.9 12.4 %copy-start.7 = (f32[384,128]{1,0:T(8,128)S(1)}, f32[384,128]{1,0:T(8,128)}, u32[]{:S(2)}) copy-start(f32[384,128]{1,0:T(8,128)} %fusion.4) | copy-start | bytes 589828
  91.9 24.0 %all-to-all-start.3 = ((f32[16,12,128]{2,1,0:T(8,128)}), f32[16,12,128]{2,1,0:T(8,128)S(1)}, u32[]{:S(2)}, u32[]{:S(2)}) async-start(f32[16,12,128]{2,1,0:T(8,128)} %get-tuple-element.5), calls=%async_computation.3 | async-start | bytes 262144 | tf_op jit(solution)/shard_map/all_to_all | solution.py:23
  119.8 5.7 %copy-start.8 = (f32[128,128]{1,0:T(8,128)S(1)}, f32[128,128]{1,0:T(8,128)}, u32[]{:S(2)}) copy-start(f32[128,128]{1,0:T(8,128)} %fusion.43) | copy-start | bytes 196612
  119.8 14.0 %all-to-all-start.4 = ((f32[32,12,128]{2,1,0:T(8,128)}), f32[32,12,128]{2,1,0:T(8,128)S(1)}, u32[]{:S(2)}, u32[]{:S(2)}) async-start(f32[32,12,128]{2,1,0:T(8,128)} %shard_map.60), calls=%async_computation.4 | async-start | bytes 524288 | tf_op jit(solution)/shard_map/all_to_all | solution.py:23
  133.8 1.0 copy-start.4
  134.8 0.7 copy-start.5
